TPU v7x, 128 devices: a whole 4x4x4 slice. The times are simulated.
128 devices in a mesh: gx: 8 (over z, core), gy: 8 (over y, x_lo), gz: 2 (over x_hi).
Axes of the slice: x: 4 (x_hi: 2, x_lo: 2; x = x_hi * 2 + x_lo), y: 4, z: 4, core: 2. Of those that a mesh axis runs over, the one named last changes fastest.
Arguments:
- grads: float32 [8, 8, 2, 16, 14336], P('gx', 'gy', 'gz'), may hold values from -100 to 100
- plan: int32 [3], replicated, may hold values from 0 to 2, each once
Outputs:
- averaged: float32 [8, 8, 2, 16, 14336], P('gx', 'gy', 'gz')
- reports: float32 [3], replicated
Inputs may be any that keep to these rules, and one draw needn't show every extreme that they name: `plan`: each of 0, 1, 2 appears once.
All inputs are finite; a program needn't handle non-finite values.
Results may differ from a plain program's by a relative error of at most 0.0003.
Values sent between devices are 32-bit elements; how exact they have to be, the bound alone decides.
No kernel may reach another device: no remote copies, remote signals or barrier semaphores. Data moves between devices by JAX's collectives and lax.ppermute only.
A program may use at most 64 MiB of HBM per device.

v0:
```python
import functools

import jax
import jax.numpy as jnp
from jax import lax
from jax.sharding import Mesh
from jax.sharding import PartitionSpec as P

GX_GY_GZ = ("gx_0", "gx_1", "gy_0", "gy_1", "gz")
GX = ("gx_0", "gx_1")
GY = ("gy_0", "gy_1")


def one_axis_at_a_time(value, axes):
    return functools.reduce(lax.pmax, axes, value)


def cut_along(value, dim, size):
    dims = value.shape
    pieces = value.reshape(*dims[:dim], size, dims[dim] // size, *dims[dim + 1 :])
    return jnp.moveaxis(pieces, dim, 0)


def summed_on_arrival(value, axis, dim):
    pieces = cut_along(value, dim, lax.axis_size(axis))
    arrived = lax.all_to_all(pieces, axis, split_axis=0, concat_axis=0, tiled=True)
    return arrived.sum(axis=0)


def copy_for_each(value, axis):
    size = lax.axis_size(axis)
    return lax.all_to_all(
        jnp.broadcast_to(value[None], (size, *value.shape)), axis, 0, 0, tiled=True
    )


def in_order(pieces, dim):
    pieces = jnp.moveaxis(pieces, 0, dim)
    dims = pieces.shape
    return pieces.reshape(*dims[:dim], dims[dim] * dims[dim + 1], *dims[dim + 2 :])


def gathered_copies(value, axis, dim):
    pieces = copy_for_each(value, axis)
    return in_order(pieces, dim)


def report(deviation):
    return one_axis_at_a_time(deviation, GX_GY_GZ)


def mean_gx(current):
    share = jax.tree.map(lambda part: summed_on_arrival(part, GX, 4), current) / lax.axis_size(GX)
    return gathered_copies(share, GX, 4)


def mean_gy(current):
    share = jax.tree.map(lambda part: summed_on_arrival(part, GY, 4), current) / lax.axis_size(GY)
    return gathered_copies(share, GY, 4)


def mean_gz(current):
    share = jax.tree.map(lambda part: summed_on_arrival(part, "gz", 4), current) / lax.axis_size(
        "gz"
    )
    return gathered_copies(share, "gz", 4)


def on_device(grads, plan):
    current = grads
    values = []
    for step in range(3):
        group = lax.switch(plan[step], [mean_gx, mean_gy, mean_gz], current)
        deviation = jnp.max(jnp.abs(current - group))
        values.append(report(deviation))
        current = group
    stacked = jnp.stack(values).astype(jnp.float32)
    return (current, stacked)


def solution(mesh):
    torus = Mesh(
        mesh.devices.reshape(4, 2, 4, 2, mesh.shape["gz"]), ("gx_0", "gx_1", "gy_0", "gy_1", "gz")
    )
    placed = (P(GX, GY, "gz", None, None), P())
    return jax.shard_map(
        on_device,
        mesh=torus,
        in_specs=placed,
        out_specs=(P(GX, GY, "gz", None, None), P()),
        check_vma=False,
    )
```

profile of v0, /device:TPU:0, one launch (start us, length us, event | category | flops | bytes accessed | tf_op | source)
XLA Modules:
  0.0 151.4 jit_solution(16370568895233903637)
XLA Ops:
  0.6 1.3 fusion
  3.8 38.7 %conditional.3 = (f32[1,1,1,16,14336]{4,3,2,1,0:T(8,128)S(1)}) conditional(s32[]{:T(128)} %bitcast.20, f32[1,1,1,16,14336]{4,3,2,1,0:T(8,128)} %param.11, f32[1,1,1,16,14336]{4,3,2,1,0:T(8,128)} %param.11, f32[1,1,1,16,14336]{4,3,2,1,0:T(8,128)} %param.11), branch_computations={%region_0.0_spmd, %region_2.0_spmd, %region_4.0_spmd} | conditional | flops 229376 | bytes 12845068 | solution.py:73
  3.9 1.5 copy.23
  5.3 0.3 copy.4
  5.6 19.8 %all_to_all.72 = f32[8,1,1,1,16,1792]{5,4,3,2,1,0:T(8,128)S(1)} all-to-all(f32[8,1,1,1,16,1792]{5,4,3,2,1,0:T(8,128)S(1)} %copy.4), channel_id=1, replica_groups=mesh['gx_0'=4,'gx_1'=2,'gy_0'=4,'gy_1'=2,'gz'=2] {'gx_0','gx_1'}, dimensions={0} | all-to-all | bytes 1835008 | tf_op jit(solution)/shard_map/cond/branch_0_fun/all_to_all | solution.py:26
  25.5 0.1 broadcast_in_dim.16
  25.6 17.0 %all_to_all.73 = f32[8,1,1,1,16,1792]{5,4,3,2,1,0:T(8,128)S(1)} all-to-all(f32[8,1,1,1,16,1792]{5,4,3,2,1,0:T(8,128)S(1)} %broadcast_in_dim.16), channel_id=1, replica_groups=mesh['gx_0'=4,'gx_1'=2,'gy_0'=4,'gy_1'=2,'gz'=2] {'gx_0','gx_1'}, dimensions={0} | all-to-all | bytes 1835008 | tf_op jit(solution)/shard_map/cond/branch_0_fun/all_to_all | solution.py:32
  42.5 0.1 copy.22
  42.6 36.0 %conditional.4 = (f32[1,1,1,16,14336]{4,3,2,1,0:T(8,128)S(1)}) conditional(s32[]{:T(128)} %bitcast.19, f32[1,1,1,16,14336]{4,3,2,1,0:T(8,128)S(1)} %get-tuple-element.44, f32[1,1,1,16,14336]{4,3,2,1,0:T(8,128)S(1)} %get-tuple-element.44, f32[1,1,1,16,14336]{4,3,2,1,0:T(8,128)S(1)} %get-tuple-element.44), branch_computations={%region_6.8_spmd, %region_8.10_spmd, %region_10.12_spmd} | conditional | flops 229376 | bytes 12845068 | solution.py:73
  42.6 0.3 copy.30
  42.9 0.3 copy.12
  43.2 19.4 %all_to_all.80 = f32[8,1,1,1,16,1792]{5,4,3,2,1,0:T(8,128)S(1)} all-to-all(f32[8,1,1,1,16,1792]{5,4,3,2,1,0:T(8,128)S(1)} %copy.12), channel_id=1, replica_groups=mesh['gx_0'=4,'gx_1'=2,'gy_0'=4,'gy_1'=2,'gz'=2] {'gy_0','gy_1'}, dimensions={0} | all-to-all | bytes 1835008 | tf_op jit(solution)/shard_map/cond/branch_1_fun/all_to_all | solution.py:26
  62.7 0.1 broadcast_in_dim.25
  62.8 15.7 %all_to_all.81 = f32[8,1,1,1,16,1792]{5,4,3,2,1,0:T(8,128)S(1)} all-to-all(f32[8,1,1,1,16,1792]{5,4,3,2,1,0:T(8,128)S(1)} %broadcast_in_dim.25), channel_id=1, replica_groups=mesh['gx_0'=4,'gx_1'=2,'gy_0'=4,'gy_1'=2,'gz'=2] {'gy_0','gy_1'}, dimensions={0} | all-to-all | bytes 1835008 | tf_op jit(solution)/shard_map/cond/branch_1_fun/all_to_all | solution.py:32
  78.5 0.1 copy.29
  78.6 0.0 copy-start
  78.6 33.8 %conditional.5 = (f32[1,1,1,16,14336]{4,3,2,1,0:T(8,128)}) conditional(s32[]{:T(128)} %bitcast.18, f32[1,1,1,16,14336]{4,3,2,1,0:T(8,128)S(1)} %get-tuple-element.45, f32[1,1,1,16,14336]{4,3,2,1,0:T(8,128)S(1)} %get-tuple-element.45, f32[1,1,1,16,14336]{4,3,2,1,0:T(8,128)S(1)} %get-tuple-element.45), branch_computations={%region_12.0_spmd, %region_14.0_spmd, %region_16.0_spmd} | conditional | flops 229376 | bytes 12845068 | solution.py:73
  78.6 1.7 %reshape.146 = f32[1,1,1,16,2,7168]{5,4,3,2,1,0:T(2,128)} reshape(f32[1,1,1,16,14336]{4,3,2,1,0:T(8,128)S(1)} %param.8) | data formatting | bytes 1835008 | tf_op jit(solution)/shard_map/cond/branch_2_fun/reshape | solution.py:20
  80.3 1.5 copy.20
  81.8 15.2 %all_to_all.88 = f32[2,1,1,1,16,7168]{5,4,3,2,1,0:T(8,128)} all-to-all(f32[2,1,1,1,16,7168]{5,4,3,2,1,0:T(8,128)S(1)} %copy.20), channel_id=1, replica_groups=mesh['gx_0'=4,'gx_1'=2,'gy_0'=4,'gy_1'=2,'gz'=2] {'gz'}, dimensions={0} | all-to-all | bytes 1835008 | tf_op jit(solution)/shard_map/cond/branch_2_fun/all_to_all | solution.py:26
  97.0 1.3 reduce_sum.80
  98.4 0.1 broadcast_in_dim.33
  98.4 12.9 %all_to_all.89 = f32[2,1,1,1,16,7168]{5,4,3,2,1,0:T(8,128)S(1)} all-to-all(f32[2,1,1,1,16,7168]{5,4,3,2,1,0:T(8,128)S(1)} %broadcast_in_dim.33), channel_id=1, replica_groups=mesh['gx_0'=4,'gx_1'=2,'gy_0'=4,'gy_1'=2,'gz'=2] {'gz'}, dimensions={0} | all-to-all | bytes 1835008 | tf_op jit(solution)/shard_map/cond/branch_2_fun/all_to_all | solution.py:32
  111.4 1.0 copy.36
  112.3 0.0 copy-done
  112.3 2.0 %abs_reduce_fusion.2 = (f32[]{:T(128)}, f32[]{:T(128)}, f32[]{:T(128)}) fusion(f32[1,1,1,16,14336]{4,3,2,1,0:T(8,128)S(1)} %copy-done, f32[1,1,1,16,14336]{4,3,2,1,0:T(8,128)S(1)} %get-tuple-element.44, f32[1,1,1,16,14336]{4,3,2,1,0:T(8,128)S(1)} %get-tuple-element.45, f32[1,1,1,16,14336]{4,3,2,1,0:T(8,128)} %get-tuple-element.46), kind=kLoop, calls=%fused_computation.11 | loop fusion | flops 2064381 | bytes 3670028 | tf_op jit(solution)/shard_map/reduce_max | solution.py:74
  114.4 9.6 %all-reduce.1 = (f32[]{:T(128)}, f32[]{:T(128)}, f32[]{:T(128)}) all-reduce(f32[]{:T(128)} %get-tuple-element.25, f32[]{:T(128)} %get-tuple-element.24, f32[]{:T(128)} %get-tuple-element.23), channel_id=1, replica_groups=mesh['gx_0'=4,'gx_1'=2,'gy_0'=4,'gy_1'=2,'gz'=2] {'gx_0'}, use_global_device_ids=true, to_apply=%region_31.0 | all-reduce | flops 3 | bytes 24 | tf_op jit(solution)/shard_map/pmax | solution.py:15
  123.9 3.1 %all-reduce.4 = (f32[]{:T(128)}, f32[]{:T(128)}, f32[]{:T(128)}) all-reduce(f32[]{:T(128)} %get-tuple-element.29, f32[]{:T(128)} %get-tuple-element.30, f32[]{:T(128)} %get-tuple-element.31), channel_id=1, replica_groups=mesh['gx_0'=4,'gx_1'=2,'gy_0'=4,'gy_1'=2,'gz'=2] {'gx_1'}, use_global_device_ids=true, to_apply=%region_32.0 | all-reduce | flops 3 | bytes 24 | tf_op jit(solution)/shard_map/pmax | solution.py:15
  127.1 9.1 %all-reduce = (f32[]{:T(128)}, f32[]{:T(128)}, f32[]{:T(128)}) all-reduce(f32[]{:T(128)} %get-tuple-element.38, f32[]{:T(128)} %get-tuple-element.39, f32[]{:T(128)} %get-tuple-element.40), channel_id=1, replica_groups=mesh['gx_0'=4,'gx_1'=2,'gy_0'=4,'gy_1'=2,'gz'=2] {'gy_0'}, use_global_device_ids=true, to_apply=%region_33.0 | all-reduce | flops 3 | bytes 24 | tf_op jit(solution)/shard_map/pmax | solution.py:15
  136.2 5.6 %all-reduce.3 = (f32[]{:T(128)}, f32[]{:T(128)}, f32[]{:T(128)}) all-reduce(f32[]{:T(128)} %get-tuple-element.26, f32[]{:T(128)} %get-tuple-element.27, f32[]{:T(128)} %get-tuple-element.28), channel_id=1, replica_groups=mesh['gx_0'=4,'gx_1'=2,'gy_0'=4,'gy_1'=2,'gz'=2] {'gy_1'}, use_global_device_ids=true, to_apply=%region_34.0 | all-reduce | flops 3 | bytes 24 | tf_op jit(solution)/shard_map/pmax | solution.py:15
  141.8 7.1 %all-reduce.2 = (f32[1]{0:T(128)}, f32[1]{0:T(128)}, f32[1]{0:T(128)}) all-reduce(f32[1]{0:T(128)} %bitcast.23, f32[1]{0:T(128)} %bitcast.22, f32[1]{0:T(128)} %bitcast.21), channel_id=1, replica_groups=mesh['gx_0'=4,'gx_1'=2,'gy_0'=4,'gy_1'=2,'gz'=2] {'gz'}, use_global_device_ids=true, to_apply=%region_35.0 | all-reduce | flops 3 | bytes 24 | tf_op jit(solution)/shard_map/pmax | solution.py:15
  148.9 2.5 %pad_maximum_fusion = f32[3]{0:T(128)} fusion(f32[1]{0:T(128)} %get-tuple-element.32, f32[1]{0:T(128)} %get-tuple-element.33, f32[1]{0:T(128)} %get-tuple-element.34), kind=kLoop, calls=%fused_computation.12 | loop fusion | flops 6 | bytes 24 | tf_op jit(solution)/shard_map/stack | solution.py:77
  (5 shorter events, 0.1 us)
Async XLA Ops:
  78.6 33.8 %copy-start = (f32[1,1,1,16,14336]{4,3,2,1,0:T(8,128)S(1)}, f32[1,1,1,16,14336]{4,3,2,1,0:T(8,128)}, u32[]{:S(2)}) copy-start(f32[1,1,1,16,14336]{4,3,2,1,0:T(8,128)} %param.11) | copy-start | bytes 2752516
where the time goes:
time: 152 us; the launch traced here: 151 us
  blocking collectives  135 us (89%)
  local copies, waits for them, and re-layouts  8.14 us (5%)
  other arithmetic  5.9 us (4%)
  between operations  2.52 us (2%)
    all_to_all x3, blocking collectives, summed_on_arrival(): lax.all_to_all(pieces, axis, split_axis=0, concat_axis=0, tiled=True)  54.4 us
    all_to_all x3, blocking collectives, copy_for_each(): lax.all_to_all(jnp.broadcast_to(value[None], (size, *value.shape)), axis,...  45.6 us
    pmax x5, blocking collectives, one_axis_at_a_time(): return functools.reduce(lax.pmax, axes, value)  34.6 us

commit v1 on v0

v1 whole, which is shorter than its diff:
```python
import jax
import jax.numpy as jnp
from jax import lax
from jax.experimental import pallas as pl
from jax.experimental.pallas import tpu as pltpu
from jax.sharding import Mesh
from jax.sharding import PartitionSpec as P

PLANE = ("z", "y", "x_lo", "x_hi")
EVERY = ("core", *PLANE)
COLS = 128
DATA = 14
CARRIED = 16
ROOM = pltpu.CompilerParams(vmem_limit_bytes=8 * 2**20)


def swap_pairs(rows, apart):
    n = rows.shape[0]
    place = lax.broadcasted_iota(jnp.int32, rows.shape, 0)
    first = (place // apart) % 2 == 0
    return jnp.where(
        first, pltpu.roll(rows, n - apart, 0), pltpu.roll(rows, apart, 0)
    )


def far(worst, value, mean):
    gap = jnp.abs(value - mean)
    return jnp.maximum(worst, jnp.max(gap.reshape(-1, 8, COLS), axis=0))


def rounds(plan_ref, g_ref, share_ref):
    zero = jnp.zeros((8, COLS), jnp.float32)
    mx = []
    for y in range(4):
        total = g_ref[y]
        for gx in range(1, 8):
            total = total + g_ref[gx * 4 + y]
        mx.append(total * 0.125)
    mxz = [(m + swap_pairs(m, DATA)) * 0.5 for m in mx]
    sum_xy = mx[0] + mx[1] + mx[2] + mx[3]
    mxy = (sum_xy + pltpu.roll(sum_xy, 2 * DATA, 0)) * 0.125
    mall = (mxy + swap_pairs(mxy, DATA)) * 0.5

    x = y_ = z = z_xz = z_yz = y_xy = y_yz = yz_all = zero
    for gx in range(8):
        part = [g_ref[gx * 4 + y] for y in range(4)]
        total = (part[0] + part[1]) + (part[2] + part[3])
        my = (total + pltpu.roll(total, 2 * DATA, 0)) * 0.125
        myz = (my + swap_pairs(my, DATA)) * 0.5
        y_xy = far(y_xy, my, mxy)
        y_yz = far(y_yz, my, myz)
        yz_all = far(yz_all, myz, mall)
        for y in range(4):
            mz = (part[y] + swap_pairs(part[y], DATA)) * 0.5
            x = far(x, part[y], mx[y])
            y_ = far(y_, part[y], my)
            z = far(z, part[y], mz)
            z_xz = far(z_xz, mz, mxz[y])
            z_yz = far(z_yz, mz, myz)
    x_xy = x_xz = xz_all = zero
    for y in range(4):
        x_xy = far(x_xy, mx[y], mxy)
        x_xz = far(x_xz, mx[y], mxz[y])
        xz_all = far(xz_all, mxz[y], mall)
    xy_all = far(zero, mxy, mall)

    a, b, c = plan_ref[0], plan_ref[1], plan_ref[2]

    def pick(which, of_x, of_y, of_z):
        return jnp.where(which == 0, of_x, jnp.where(which == 1, of_y, of_z))

    first = pick(a, x, y_, z)
    second = pick(
        a,
        jnp.where(b == 1, x_xy, x_xz),
        jnp.where(b == 0, y_xy, y_yz),
        jnp.where(b == 0, z_xz, z_yz),
    )
    third = pick(c, yz_all, xz_all, xy_all)
    lane = lax.broadcasted_iota(jnp.int32, (2, COLS), 1)
    told = jnp.where(
        lane == 0,
        jnp.max(first),
        jnp.where(lane == 1, jnp.max(second), jnp.max(third)),
    )
    share = jnp.concatenate([mall[:DATA], told], axis=0)
    for i in range(share_ref.shape[0]):
        share_ref[i] = share


def spread(own_ref, other_ref, out_ref, reports_ref, sems):
    core = lax.axis_index("core")
    count = own_ref.shape[0]
    copies = []
    for i, (half, side) in enumerate(((own_ref, core), (other_ref, 1 - core))):
        place = out_ref.at[pl.ds(side * count, count)]
        copies.append(
            pltpu.make_async_copy(half.at[:, : DATA // 2], place, sems.at[i])
        )
        copies[-1].start()
    worst = jnp.maximum(
        jnp.max(own_ref[:, DATA // 2], axis=0),
        jnp.max(other_ref[:, DATA // 2], axis=0),
    )
    lane = lax.broadcasted_iota(jnp.int32, worst.shape, 1)
    for r in range(3):
        reports_ref[r] = jnp.max(jnp.where(lane == r, worst, 0.0))
    for copy in copies:
        copy.wait()


def on_device(grads, plan):
    rows, width = grads.shape[-2:]
    tiles = width // COLS
    count = lax.axis_size(EVERY)
    entries = grads.reshape(rows // 8, 8, tiles, COLS).transpose(0, 2, 1, 3)
    entries = entries.reshape(count, DATA // 2, 2, COLS)
    arrived = lax.all_to_all(entries, EVERY, 0, 0, tiled=True)
    peers = lax.axis_size(PLANE)
    share = pl.pallas_call(
        rounds,
        out_shape=jax.ShapeDtypeStruct((peers, CARRIED, COLS), jnp.float32),
        in_specs=[
            pl.BlockSpec(memory_space=pltpu.SMEM),
            pl.BlockSpec(memory_space=pltpu.VMEM),
        ],
        out_specs=pl.BlockSpec(memory_space=pltpu.VMEM),
        compiler_params=ROOM,
    )(plan, arrived.reshape(count // 4, 4 * DATA, COLS))
    half = lax.all_to_all(share, PLANE, 0, 0, tiled=True)
    half = half.reshape(peers, CARRIED // 2, 2, COLS)
    other = lax.ppermute(half, "core", [(0, 1), (1, 0)])
    whole, reports = pl.pallas_call(
        spread,
        out_shape=(
            jax.ShapeDtypeStruct((count, DATA // 2, 2, COLS), jnp.float32),
            jax.ShapeDtypeStruct((3,), jnp.float32),
        ),
        in_specs=[pl.BlockSpec(memory_space=pltpu.VMEM)] * 2,
        out_specs=(
            pl.BlockSpec(memory_space=pl.ANY),
            pl.BlockSpec(memory_space=pltpu.SMEM),
        ),
        scratch_shapes=[pltpu.SemaphoreType.DMA((2,))],
        compiler_params=ROOM,
    )(half, other)
    whole = whole.reshape(rows // 8, tiles, 8, COLS).transpose(0, 2, 1, 3)
    return whole.reshape(grads.shape), reports


def solution(mesh):
    torus = Mesh(
        mesh.devices.reshape(4, 2, 4, 2, mesh.shape["gz"]),
        ("z", "core", "y", "x_lo", "x_hi"),
    )
    placed = P(("z", "core"), ("y", "x_lo"), "x_hi", None, None)
    return jax.shard_map(
        on_device,
        mesh=torus,
        in_specs=(placed, P()),
        out_specs=(placed, P()),
        check_vma=False,
    )
```

time: 152 us -> 54.9 us (0.36)
  the two profiles are of different devices: /device:TPU:0 before, /device:TPU:1 now
where the time goes in v1:
time: 54.9 us; the launch traced here: 54.7 us
  blocking collectives  46.9 us (85%)
  Pallas kernels  3.16 us (6%)
  starting transfers between devices  1.84 us (3%)
  waiting for transfers between devices  1.54 us (3%)
  local copies, waits for them, and re-layouts  0.66 us (1%)
  between operations  0.64 us (1%)
    all_to_all x1, blocking collectives, on_device(): arrived = lax.all_to_all(entries, EVERY, 0, 0, tiled=True)  29.3 us
    all_to_all x1, blocking collectives, on_device(): half = lax.all_to_all(share, PLANE, 0, 0, tiled=True)  17.6 us
    ppermute x1, starting transfers between devices, on_device(): other = lax.ppermute(half, 'core', [(0, 1), (1, 0)])  1.84 us
    pallas_call x1, Pallas kernels, on_device(): pl.pallas_call(rounds, out_shape=jax.ShapeDtypeStruct((peers, CARRIED, CO...  1.66 us
    ppermute x1, waiting for transfers between devices, on_device(): other = lax.ppermute(half, 'core', [(0, 1), (1, 0)])  1.54 us
    pallas_call x1, Pallas kernels, on_device(): pl.pallas_call(spread, out_shape=(jax.ShapeDtypeStruct((count, DATA // 2,...  1.49 us
  transfers between devices with their start and end apart: 1, of which 1 were waited for; matrix products, arithmetic and copies ran while one was open for 0% of the time, Pallas kernels for 0%

profile of v1, /device:TPU:1, one launch (start us, length us, event | category | flops | bytes accessed | tf_op | source)
XLA Modules:
  0.0 54.7 jit_solution(17509068403670397108)
XLA Ops:
  0.6 29.3 %all_to_all.10 = f32[128,7,2,128]{3,2,1,0:T(2,128)S(1)} all-to-all(f32[128,7,2,128]{3,2,1,0:T(2,128)} %bitcast.15), channel_id=1, replica_groups=mesh['z'=4,'core'=2,'y'=4,'x_lo'=2,'x_hi'=2] {'core','z','y','x_lo','x_hi'}, dimensions={0} | all-to-all | bytes 1835008 | tf_op jit(solution)/shard_map/all_to_all | solution.py:118
  29.9 0.0 copy-start
  29.9 0.7 %copy-done = s32[3]{0:T(128)S(1)} copy-done((s32[3]{0:T(128)S(1)}, s32[3]{0:T(128)}, u32[]{:S(2)}) %copy-start) | copy-done | bytes 36
  30.6 1.7 %shard_map.41 = f32[64,16,128]{2,1,0:T(8,128)S(1)} custom-call(s32[3]{0:T(128)S(1)} %copy-done, f32[32,56,128]{2,1,0:T(8,128)S(1)} %bitcast.12), custom_call_target="tpu_custom_call" | custom-call | tf_op jit(solution)/shard_map/pallas_call | solution.py:120
  32.2 17.6 %all_to_all.11 = f32[64,16,128]{2,1,0:T(8,128)S(1)} all-to-all(f32[64,16,128]{2,1,0:T(8,128)S(1)} %shard_map.41), channel_id=1, replica_groups=mesh['z'=4,'core'=2,'y'=4,'x_lo'=2,'x_hi'=2] {'z','y','x_lo','x_hi'}, dimensions={0} | all-to-all | bytes 1048576 | tf_op jit(solution)/shard_map/all_to_all | solution.py:130
  49.8 1.8 %collective-permute-start = (f32[64,8,2,128]{3,2,1,0:T(2,128)S(1)}, f32[64,8,2,128]{3,2,1,0:T(2,128)S(1)}, u32[]{:S(2)}, u32[]{:S(2)}) collective-permute-start(f32[64,8,2,128]{3,2,1,0:T(2,128)S(1)} %bitcast.13), channel_id=1, source_target_pairs={{0,16},{16,0},{1,17},{17,1},{2,18},{18,2},{3,19},{19,3},{4,20},{20... | collective-permute-start | bytes 1572872 | tf_op jit(solution)/shard_map/ppermute | solution.py:132
  51.7 1.5 %collective-permute-done.other_ref = f32[64,8,2,128]{3,2,1,0:T(2,128)S(1)} collective-permute-done((f32[64,8,2,128]{3,2,1,0:T(2,128)S(1)}, f32[64,8,2,128]{3,2,1,0:T(2,128)S(1)}, u32[]{:S(2)}, u32[]{:S(2)}) %collective-permute-start) | collective-permute-done | bytes 524320 | tf_op jit(solution)/shard_map/ppermute | solution.py:132
  53.2 1.5 %shard_map.42 = (f32[128,7,2,128]{3,2,1,0:T(2,128)}, f32[3]{0:T(128)}) custom-call(f32[64,8,2,128]{3,2,1,0:T(2,128)S(1)} %bitcast.14, f32[64,8,2,128]{3,2,1,0:T(2,128)S(1)} %collective-permute-done.other_ref), custom_call_target="tpu_custom_call" | custom-call | tf_op jit(solution)/shard_map/pallas_call | solution.py:133
Async XLA Ops:
  29.9 0.7 %copy-start = (s32[3]{0:T(128)S(1)}, s32[3]{0:T(128)}, u32[]{:S(2)}) copy-start(s32[3]{0:T(128)} %plan_ref.1) | copy-start | bytes 40
  49.8 3.4 %collective-permute-start = (f32[64,8,2,128]{3,2,1,0:T(2,128)S(1)}, f32[64,8,2,128]{3,2,1,0:T(2,128)S(1)}, u32[]{:S(2)}, u32[]{:S(2)}) collective-permute-start(f32[64,8,2,128]{3,2,1,0:T(2,128)S(1)} %bitcast.13), channel_id=1, source_target_pairs={{0,16},{16,0},{1,17},{17,1},{2,18},{18,2},{3,19},{19,3},{4,20},{20... | collective-permute-start | bytes 1572872 | tf_op jit(solution)/shard_map/ppermute | solution.py:132

commit v2 on v0

v2 whole, which is shorter than its diff:
```python
import jax
import jax.numpy as jnp
from jax import lax
from jax.experimental import pallas as pl
from jax.experimental.pallas import tpu as pltpu
from jax.sharding import Mesh
from jax.sharding import PartitionSpec as P

PLANE = ("y", "z", "x_hi", "x_lo")
EVERY = ("core", *PLANE)
COLS = 128
DATA = 14
CARRIED = 16
TILES = 4 * DATA // 8
UPPER = 4
SLOT = COLS // 8
ROOM = pltpu.CompilerParams(vmem_limit_bytes=8 * 2**20)


def both_ways(high, low, mean):
    return jnp.maximum(high - mean, mean - low)


def stats(values):
    total = high = low = values[0]
    for value in values[1:]:
        total = total + value
        high = jnp.maximum(high, value)
        low = jnp.minimum(low, value)
    return total, high, low


def rows_of(tiles):
    return jnp.concatenate(tiles, axis=0)


def tiles_of(rows):
    return [rows[8 * t : 8 * t + 8] for t in range(rows.shape[0] // 8)]


def across_x_hi(tiles):
    turned = {t: pltpu.roll(tiles[t], 4, 0) for t in (0, 3, 4, 5, 6)}
    first = lax.broadcasted_iota(jnp.int32, (8, COLS), 0) < 4
    return [
        jnp.where(first, turned[t + 3], turned[(t + 4) % TILES])
        for t in range(UPPER)
    ]


def across_x_lo(tiles):
    rows = rows_of(tiles)
    n = rows.shape[0]
    place = lax.broadcasted_iota(jnp.int32, rows.shape, 0)
    first = ((place >= 0) & (place < DATA)) | (
        (place >= 2 * DATA) & (place < 3 * DATA)
    )
    return tiles_of(
        jnp.where(
            first, pltpu.roll(rows, n - DATA, 0), pltpu.roll(rows, DATA, 0)
        )
    )


def most(values):
    worst = values[0]
    for value in values[1:]:
        worst = jnp.maximum(worst, value)
    return worst


def gaps(tiles, means):
    return [jnp.abs(t - m) for t, m in zip(tiles, means)]


def packed(eight):
    worst = rows_of([jnp.max(v, axis=0, keepdims=True) for v in eight])
    for apart in (64, 32, 16):
        worst = jnp.maximum(worst, pltpu.roll(worst, apart, 1))
    row = lax.broadcasted_iota(jnp.int32, worst.shape, 0)
    lane = lax.broadcasted_iota(jnp.int32, worst.shape, 1)
    return jnp.max(
        jnp.where(row == lane // SLOT, worst, 0.0), axis=0, keepdims=True
    )


def rounds(g_ref, share_ref):
    where = {
        (gx, y): (gx // 4) * 16 + y * 4 + gx % 4
        for gx in range(8)
        for y in range(4)
    }
    half = lambda tiles: [t * 0.5 for t in tiles]
    mx, dev_x = [None] * 4, []
    my_sum, y_high, y_low = [[] for _ in range(8)], [], []
    load = lambda gx, y, t: g_ref[where[gx, y], 8 * t : 8 * t + 8]

    dev_z = []
    mz_of_y = [[[] for _ in range(UPPER)] for _ in range(4)]
    mz_of_gx = [[[] for _ in range(UPPER)] for _ in range(8)]
    for y in range(4):
        x_stats = []
        for t in range(TILES):
            x_stats.append(stats([load(gx, y, t) for gx in range(8)]))
        mx[y] = [s[0] * 0.125 for s in x_stats]
        dev_x += [both_ways(s[1], s[2], m) for s, m in zip(x_stats, mx[y])]
        for gx in range(8):
            tiles = [load(gx, y, t) for t in range(TILES)]
            for t, other in enumerate(across_x_hi(tiles)):
                mean = (tiles[t] + other) * 0.5
                dev_z.append(jnp.abs(tiles[t] - mean))
                mz_of_y[y][t].append(mean)
                mz_of_gx[gx][t].append(mean)
        dev_x, dev_z = [most(dev_x)], [most(dev_z)]

    my, dev_y = [], []
    for gx in range(8):
        y_stats = [
            stats([load(gx, y, t) for y in range(4)]) for t in range(TILES)
        ]
        total = [s[0] for s in y_stats]
        my.append([(a + b) * 0.125 for a, b in zip(total, across_x_lo(total))])
        dev_y += [both_ways(s[1], s[2], m) for s, m in zip(y_stats, my[gx])]
        dev_y = [most(dev_y)]

    def with_other(tiles):
        return [(a + b) * 0.5 for a, b in zip(tiles, across_x_hi(tiles))]

    mxz = [with_other(m) for m in mx]
    myz = [with_other(m) for m in my]
    mxy = [stats([my[gx][t] for gx in range(8)])[0] * 0.125 for t in range(TILES)]
    mall = with_other(mxy)

    x_xy = most([most(gaps(mx[y], mxy)) for y in range(4)])
    x_xz = most([most(gaps(mx[y][:UPPER], mxz[y])) for y in range(4)])
    y_xy = most([most(gaps(my[gx], mxy)) for gx in range(8)])
    y_yz = most([most(gaps(my[gx][:UPPER], myz[gx])) for gx in range(8)])

    def spread_of(values, means):
        worst = []
        for t in range(UPPER):
            _, high, low = stats(values[t])
            worst.append(both_ways(high, low, means[t]))
        return most(worst)

    z_xz = most([spread_of(mz_of_y[y], mxz[y]) for y in range(4)])
    z_yz = most([spread_of(mz_of_gx[gx], myz[gx]) for gx in range(8)])
    xy_all = most(gaps(mxy[:UPPER], mall))
    xz_all = most([most(gaps(mxz[y], mall)) for y in range(4)])
    yz_all = most([most(gaps(myz[gx], mall)) for gx in range(8)])

    none = jnp.zeros((8, COLS), jnp.float32)
    slots = [dev_x[0], dev_y[0], dev_z[0]]
    slots += [none, x_xy, x_xz, y_xy, none, y_yz, z_xz, z_yz, none]
    slots += [yz_all, xz_all, xy_all, none]
    told = rows_of([packed(slots[:8]), packed(slots[8:])])
    share = jnp.concatenate([rows_of(mall[:2])[:DATA], told], axis=0)
    for i in range(share_ref.shape[0]):
        share_ref[i] = share


def place(half_ref, out_ref, side, sem):
    count = half_ref.shape[0]
    return pltpu.make_async_copy(
        half_ref.at[:, : DATA // 2],
        out_ref.at[pl.ds(side * count, count)],
        sem,
    )


def put_own(own_ref, out_ref, sem):
    copy = place(own_ref, out_ref, lax.axis_index("core"), sem)
    copy.start()
    copy.wait()


def put_other(
    plan_ref, own_ref, other_ref, _, out_ref, reports_ref, plan_here, sems
):
    asked = pltpu.make_async_copy(plan_ref, plan_here, sems.at[1])
    asked.start()
    copy = place(other_ref, out_ref, 1 - lax.axis_index("core"), sems.at[0])
    copy.start()
    worst = jnp.maximum(
        jnp.max(own_ref[:, DATA // 2], axis=0),
        jnp.max(other_ref[:, DATA // 2], axis=0),
    )
    row = lax.broadcasted_iota(jnp.int32, worst.shape, 0)
    lane = lax.broadcasted_iota(jnp.int32, worst.shape, 1)
    slot = 8 * row + lane // SLOT
    asked.wait()
    a, b, c = plan_here[0], plan_here[1], plan_here[2]
    for r, wanted in enumerate((a, 3 + 3 * a + b, 12 + c)):
        reports_ref[r] = jnp.max(jnp.where(slot == wanted, worst, 0.0))
    copy.wait()


def on_device(grads, plan):
    rows, width = grads.shape[-2:]
    tiles = width // COLS
    count = lax.axis_size(EVERY)
    vmem = pl.BlockSpec(memory_space=pltpu.VMEM)
    smem = pl.BlockSpec(memory_space=pltpu.SMEM)
    hbm = pl.BlockSpec(memory_space=pl.ANY)
    entries = grads.reshape(rows // 8, 8, tiles, COLS).transpose(0, 2, 1, 3)
    entries = entries.reshape(count, DATA // 2, 2, COLS)
    arrived = lax.all_to_all(entries, EVERY, 0, 0, tiled=True)
    peers = lax.axis_size(PLANE)
    share = pl.pallas_call(
        rounds,
        out_shape=jax.ShapeDtypeStruct((peers, CARRIED, COLS), jnp.float32),
        in_specs=[vmem],
        out_specs=vmem,
        compiler_params=ROOM,
    )(arrived.reshape(count // 4, 4 * DATA, COLS))
    own = lax.all_to_all(share, PLANE, 0, 0, tiled=True)
    own = own.reshape(peers, CARRIED // 2, 2, COLS)
    other = lax.ppermute(own, "core", [(0, 1), (1, 0)])
    whole_type = jax.ShapeDtypeStruct((count, DATA // 2, 2, COLS), jnp.float32)
    cost = pl.CostEstimate(
        flops=10**7, bytes_accessed=own.size * 4, transcendentals=0
    )
    begun = pl.pallas_call(
        put_own,
        out_shape=whole_type,
        in_specs=[vmem],
        out_specs=hbm,
        scratch_shapes=[pltpu.SemaphoreType.DMA],
        compiler_params=ROOM,
        cost_estimate=cost,
    )(own)
    whole, reports = pl.pallas_call(
        put_other,
        out_shape=(whole_type, jax.ShapeDtypeStruct((3,), jnp.float32)),
        in_specs=[hbm, vmem, vmem, hbm],
        out_specs=(hbm, smem),
        scratch_shapes=[
            pltpu.SMEM(plan.shape, plan.dtype),
            pltpu.SemaphoreType.DMA((2,)),
        ],
        input_output_aliases={3: 0},
        compiler_params=ROOM,
    )(plan, own, other, begun)
    whole = whole.reshape(rows // 8, tiles, 8, COLS).transpose(0, 2, 1, 3)
    return whole.reshape(grads.shape), reports


def solution(mesh):
    torus = Mesh(
        mesh.devices.reshape(4, 2, 4, 2, mesh.shape["gz"]),
        ("z", "core", "y", "x_lo", "x_hi"),
    )
    placed = P(("z", "core"), ("y", "x_lo"), "x_hi", None, None)
    return jax.shard_map(
        on_device,
        mesh=torus,
        in_specs=(placed, P()),
        out_specs=(placed, P()),
        check_vma=False,
    )
```

time: 152 us -> 52.9 us (0.35)
  the two profiles are of different devices: /device:TPU:0 before, /device:TPU:1 now
where the time goes in v2:
time: 52.9 us; the launch traced here: 52.7 us
  blocking collectives  46.3 us (88%)
  Pallas kernels  2.98 us (6%)
  starting transfers between devices  2.01 us (4%)
  waiting for transfers between devices  0.75 us (1%)
  between operations  0.65 us (1%)
    all_to_all x1, blocking collectives, on_device(): arrived = lax.all_to_all(entries, EVERY, 0, 0, tiled=True)  28.8 us
    all_to_all x1, blocking collectives, on_device(): own = lax.all_to_all(share, PLANE, 0, 0, tiled=True)  17.5 us
    ppermute x1, starting transfers between devices, on_device(): other = lax.ppermute(own, 'core', [(0, 1), (1, 0)])  2.01 us
    pallas_call x1, Pallas kernels, on_device(): pl.pallas_call(put_other, out_shape=(whole_type, jax.ShapeDtypeStruct((3,...  1.31 us
  transfers between devices with their start and end apart: 1, of which 1 were waited for; matrix products, arithmetic and copies ran while one was open for 0% of the time, Pallas kernels for 1%

profile of v2, /device:TPU:1, one launch (start us, length us, event | category | flops | bytes accessed | tf_op | source)
XLA Modules:
  0.0 52.7 jit_solution(14010555376476755133)
XLA Ops:
  0.6 28.8 %all_to_all.10 = f32[128,7,2,128]{3,2,1,0:T(2,128)S(1)} all-to-all(f32[128,7,2,128]{3,2,1,0:T(2,128)} %bitcast.17), channel_id=1, replica_groups=mesh['z'=4,'core'=2,'y'=4,'x_lo'=2,'x_hi'=2] {'core','y','z','x_hi','x_lo'}, dimensions={0} | all-to-all | bytes 1835008 | tf_op jit(solution)/shard_map/all_to_all | solution.py:206
  29.4 0.9 %shard_map.41 = f32[64,16,128]{2,1,0:T(8,128)S(1)} custom-call(f32[32,56,128]{2,1,0:T(8,128)S(1)} %bitcast.15), custom_call_target="tpu_custom_call" | custom-call | tf_op jit(solution)/shard_map/pallas_call | solution.py:208
  30.3 17.5 %all_to_all.11 = f32[64,16,128]{2,1,0:T(8,128)S(1)} all-to-all(f32[64,16,128]{2,1,0:T(8,128)S(1)} %shard_map.41), channel_id=1, replica_groups=mesh['z'=4,'core'=2,'y'=4,'x_lo'=2,'x_hi'=2] {'y','z','x_hi','x_lo'}, dimensions={0} | all-to-all | bytes 1048576 | tf_op jit(solution)/shard_map/all_to_all | solution.py:215
  47.8 0.0 copy-start
  47.8 2.0 %collective-permute-start = (f32[64,8,2,128]{3,2,1,0:T(2,128)S(1)}, f32[64,8,2,128]{3,2,1,0:T(2,128)S(1)}, u32[]{:S(2)}, u32[]{:S(2)}) collective-permute-start(f32[64,8,2,128]{3,2,1,0:T(2,128)S(1)} %bitcast.12), channel_id=1, source_target_pairs={{0,16},{16,0},{1,17},{17,1},{2,18},{18,2},{3,19},{19,3},{4,20},{20... | collective-permute-start | bytes 1572872 | tf_op jit(solution)/shard_map/ppermute | solution.py:217
  49.8 0.8 %shard_map.42._ = f32[128,7,2,128]{3,2,1,0:T(2,128)} custom-call(f32[64,8,2,128]{3,2,1,0:T(2,128)S(1)} %bitcast.13), custom_call_target="tpu_custom_call" | custom-call | flops 10000000 | bytes 524288 | tf_op jit(solution)/shard_map/pallas_call | solution.py:222
  50.6 0.8 %collective-permute-done.other_ref = f32[64,8,2,128]{3,2,1,0:T(2,128)S(1)} collective-permute-done((f32[64,8,2,128]{3,2,1,0:T(2,128)S(1)}, f32[64,8,2,128]{3,2,1,0:T(2,128)S(1)}, u32[]{:S(2)}, u32[]{:S(2)}) %collective-permute-start) | collective-permute-done | bytes 524320 | tf_op jit(solution)/shard_map/ppermute | solution.py:217
  51.4 0.0 copy-done
  51.4 1.3 %shard_map.43 = (f32[128,7,2,128]{3,2,1,0:T(2,128)}, f32[3]{0:T(128)}) custom-call(s32[3]{0:T(128)S(1)} %copy-done, f32[64,8,2,128]{3,2,1,0:T(2,128)S(1)} %bitcast.14, f32[64,8,2,128]{3,2,1,0:T(2,128)S(1)} %collective-permute-done.other_ref, f32[128,7,2,128]{3,2,1,0:T(2,128)} %shard_map.42._), custom_call_target="tpu_custom_call", output_to_operand_aliasing={{0}: (3, {})} | custom-call | tf_op jit(solution)/shard_map/pallas_call | solution.py:231
Async XLA Ops:
  47.8 3.6 %copy-start = (s32[3]{0:T(128)S(1)}, s32[3]{0:T(128)}, u32[]{:S(2)}) copy-start(s32[3]{0:T(128)} %plan_ref.1) | copy-start | bytes 40
  47.8 3.6 %collective-permute-start = (f32[64,8,2,128]{3,2,1,0:T(2,128)S(1)}, f32[64,8,2,128]{3,2,1,0:T(2,128)S(1)}, u32[]{:S(2)}, u32[]{:S(2)}) collective-permute-start(f32[64,8,2,128]{3,2,1,0:T(2,128)S(1)} %bitcast.12), channel_id=1, source_target_pairs={{0,16},{16,0},{1,17},{17,1},{2,18},{18,2},{3,19},{19,3},{4,20},{20... | collective-permute-start | bytes 1572872 | tf_op jit(solution)/shard_map/ppermute | solution.py:217

commit v3 on v2

--- a/solution.py
+++ b/solution.py
@@ -1,3 +1,5 @@
+import functools
+
 import jax
 import jax.numpy as jnp
 from jax import lax
@@ -158,40 +160,56 @@
         share_ref[i] = share
 
 
-def place(half_ref, out_ref, side, sem):
+def begin(half_ref, out_ref, side, sems):
     count = half_ref.shape[0]
-    return pltpu.make_async_copy(
-        half_ref.at[:, : DATA // 2],
-        out_ref.at[pl.ds(side * count, count)],
-        sem,
-    )
-
-
-def put_own(own_ref, out_ref, sem):
-    copy = place(own_ref, out_ref, lax.axis_index("core"), sem)
-    copy.start()
-    copy.wait()
-
-
-def put_other(
-    plan_ref, own_ref, other_ref, _, out_ref, reports_ref, plan_here, sems
+    part = count // sems.shape[0]
+    copies = [
+        pltpu.make_async_copy(
+            half_ref.at[pl.ds(i * part, part), : DATA // 2],
+            out_ref.at[pl.ds(side * count + i * part, part)],
+            sems.at[i],
+        )
+        for i in range(sems.shape[0])
+    ]
+    for copy in copies:
+        copy.start()
+    return copies
+
+
+def put_own(
+    plan_ref, own_ref, out_ref, worst_ref, asked_ref, plan_here, sems, plan_sem
 ):
-    asked = pltpu.make_async_copy(plan_ref, plan_here, sems.at[1])
+    asked = pltpu.make_async_copy(plan_ref, plan_here, plan_sem)
     asked.start()
-    copy = place(other_ref, out_ref, 1 - lax.axis_index("core"), sems.at[0])
-    copy.start()
-    worst = jnp.maximum(
-        jnp.max(own_ref[:, DATA // 2], axis=0),
-        jnp.max(other_ref[:, DATA // 2], axis=0),
-    )
+    copies = begin(own_ref, out_ref, lax.axis_index("core"), sems)
+    worst = jnp.max(own_ref[:, DATA // 2], axis=0)
+    worst_ref[...] = worst
     row = lax.broadcasted_iota(jnp.int32, worst.shape, 0)
     lane = lax.broadcasted_iota(jnp.int32, worst.shape, 1)
     slot = 8 * row + lane // SLOT
     asked.wait()
     a, b, c = plan_here[0], plan_here[1], plan_here[2]
     for r, wanted in enumerate((a, 3 + 3 * a + b, 12 + c)):
-        reports_ref[r] = jnp.max(jnp.where(slot == wanted, worst, 0.0))
-    copy.wait()
+        asked_ref[r] = jnp.where(slot == wanted, 1.0, 0.0)
+    for copy in copies:
+        copy.wait()
+
+
+def put_other(
+    worst_ref, asked_ref, other_ref, _, out_ref, reports_ref,
+    reports_here, sems, reports_sem,
+):
+    copies = begin(other_ref, out_ref, 1 - lax.axis_index("core"), sems)
+    worst = jnp.maximum(
+        worst_ref[...], jnp.max(other_ref[:, DATA // 2], axis=0)
+    )
+    for r in range(3):
+        wanted = asked_ref[r] > 0.0
+        reports_here[r] = jnp.max(jnp.where(wanted, worst, 0.0))
+    told = pltpu.make_async_copy(reports_here, reports_ref, reports_sem)
+    told.start()
+    for copy in (*copies, told):
+        copy.wait()
 
 
 def on_device(grads, plan):
@@ -199,7 +217,6 @@
     tiles = width // COLS
     count = lax.axis_size(EVERY)
     vmem = pl.BlockSpec(memory_space=pltpu.VMEM)
-    smem = pl.BlockSpec(memory_space=pltpu.SMEM)
     hbm = pl.BlockSpec(memory_space=pl.ANY)
     entries = grads.reshape(rows // 8, 8, tiles, COLS).transpose(0, 2, 1, 3)
     entries = entries.reshape(count, DATA // 2, 2, COLS)
@@ -219,27 +236,33 @@
     cost = pl.CostEstimate(
         flops=10**7, bytes_accessed=own.size * 4, transcendentals=0
     )
-    begun = pl.pallas_call(
+    real = functools.partial(jax.ShapeDtypeStruct, dtype=jnp.float32)
+    begun, worst, asked = pl.pallas_call(
         put_own,
-        out_shape=whole_type,
-        in_specs=[vmem],
-        out_specs=hbm,
-        scratch_shapes=[pltpu.SemaphoreType.DMA],
+        out_shape=(whole_type, real((2, COLS)), real((3, 2, COLS))),
+        in_specs=[hbm, vmem],
+        out_specs=(hbm, vmem, vmem),
+        scratch_shapes=[
+            pltpu.SMEM(plan.shape, plan.dtype),
+            pltpu.SemaphoreType.DMA((4,)),
+            pltpu.SemaphoreType.DMA,
+        ],
         compiler_params=ROOM,
         cost_estimate=cost,
-    )(own)
+    )(plan, own)
     whole, reports = pl.pallas_call(
         put_other,
-        out_shape=(whole_type, jax.ShapeDtypeStruct((3,), jnp.float32)),
-        in_specs=[hbm, vmem, vmem, hbm],
-        out_specs=(hbm, smem),
+        out_shape=(whole_type, real((3,))),
+        in_specs=[vmem, vmem, vmem, hbm],
+        out_specs=(hbm, hbm),
         scratch_shapes=[
-            pltpu.SMEM(plan.shape, plan.dtype),
-            pltpu.SemaphoreType.DMA((2,)),
+            pltpu.SMEM((3,), jnp.float32),
+            pltpu.SemaphoreType.DMA((4,)),
+            pltpu.SemaphoreType.DMA,
         ],
         input_output_aliases={3: 0},
         compiler_params=ROOM,
-    )(plan, own, other, begun)
+    )(worst, asked, other, begun)
     whole = whole.reshape(rows // 8, tiles, 8, COLS).transpose(0, 2, 1, 3)
     return whole.reshape(grads.shape), reports
 

time: 52.9 us -> 52.4 us (level)
  transfers between devices with their start and end apart: 1 -> 1, of which waited for: 1 -> 1; matrix products, arithmetic and copies ran while one was open for 0% -> 0% of each run, Pallas kernels for 1% -> 2%
where the time goes in v3:
time: 52.4 us; the launch traced here: 52.2 us
  blocking collectives  46.3 us (88%)
  Pallas kernels  2.54 us (5%)
  starting transfers between devices  2.01 us (4%)
  waiting for transfers between devices  0.71 us (1%)
  between operations  0.65 us (1%)
    all_to_all x1, blocking collectives, on_device(): arrived = lax.all_to_all(entries, EVERY, 0, 0, tiled=True)  28.8 us
    all_to_all x1, blocking collectives, on_device(): own = lax.all_to_all(share, PLANE, 0, 0, tiled=True)  17.5 us
    ppermute x1, starting transfers between devices, on_device(): other = lax.ppermute(own, 'core', [(0, 1), (1, 0)])  2.01 us
  transfers between devices with their start and end apart: 1, of which 1 were waited for; matrix products, arithmetic and copies ran while one was open for 0% of the time, Pallas kernels for 2%

profile of v3, /device:TPU:1, one launch (start us, length us, event | category | flops | bytes accessed | tf_op | source)
XLA Modules:
  0.0 52.2 jit_solution(8727700947194760059)
XLA Ops:
  0.6 28.8 %all_to_all.10 = f32[128,7,2,128]{3,2,1,0:T(2,128)S(1)} all-to-all(f32[128,7,2,128]{3,2,1,0:T(2,128)} %bitcast.15), channel_id=1, replica_groups=mesh['z'=4,'core'=2,'y'=4,'x_lo'=2,'x_hi'=2] {'core','y','z','x_hi','x_lo'}, dimensions={0} | all-to-all | bytes 1835008 | tf_op jit(solution)/shard_map/all_to_all | solution.py:223
  29.4 0.9 %shard_map.41 = f32[64,16,128]{2,1,0:T(8,128)S(1)} custom-call(f32[32,56,128]{2,1,0:T(8,128)S(1)} %bitcast.12), custom_call_target="tpu_custom_call" | custom-call | tf_op jit(solution)/shard_map/pallas_call | solution.py:225
  30.3 17.5 %all_to_all.11 = f32[64,16,128]{2,1,0:T(8,128)S(1)} all-to-all(f32[64,16,128]{2,1,0:T(8,128)S(1)} %shard_map.41), channel_id=1, replica_groups=mesh['z'=4,'core'=2,'y'=4,'x_lo'=2,'x_hi'=2] {'y','z','x_hi','x_lo'}, dimensions={0} | all-to-all | bytes 1048576 | tf_op jit(solution)/shard_map/all_to_all | solution.py:232
  47.8 0.0 copy-start
  47.8 2.0 %collective-permute-start = (f32[64,8,2,128]{3,2,1,0:T(2,128)S(1)}, f32[64,8,2,128]{3,2,1,0:T(2,128)S(1)}, u32[]{:S(2)}, u32[]{:S(2)}) collective-permute-start(f32[64,8,2,128]{3,2,1,0:T(2,128)S(1)} %bitcast.13), channel_id=1, source_target_pairs={{0,16},{16,0},{1,17},{17,1},{2,18},{18,2},{3,19},{19,3},{4,20},{20... | collective-permute-start | bytes 1572872 | tf_op jit(solution)/shard_map/ppermute | solution.py:234
  49.8 0.0 copy-done
  49.8 0.8 %shard_map.42 = (f32[128,7,2,128]{3,2,1,0:T(2,128)}, f32[2,128]{1,0:T(2,128)S(1)}, f32[3,2,128]{2,1,0:T(2,128)S(1)}) custom-call(s32[3]{0:T(128)S(1)} %copy-done, f32[64,8,2,128]{3,2,1,0:T(2,128)S(1)} %bitcast.14), custom_call_target="tpu_custom_call" | custom-call | flops 10000000 | bytes 524288 | tf_op jit(solution)/shard_map/pallas_call | solution.py:240
  50.6 0.7 %collective-permute-done.other_ref = f32[64,8,2,128]{3,2,1,0:T(2,128)S(1)} collective-permute-done((f32[64,8,2,128]{3,2,1,0:T(2,128)S(1)}, f32[64,8,2,128]{3,2,1,0:T(2,128)S(1)}, u32[]{:S(2)}, u32[]{:S(2)}) %collective-permute-start) | collective-permute-done | bytes 524320 | tf_op jit(solution)/shard_map/ppermute | solution.py:234
  51.4 0.8 %shard_map.43 = (f32[128,7,2,128]{3,2,1,0:T(2,128)}, f32[3]{0:T(128)}) custom-call(f32[2,128]{1,0:T(2,128)S(1)} %get-tuple-element.7.worst_ref, f32[3,2,128]{2,1,0:T(2,128)S(1)} %get-tuple-element.8.asked_ref, f32[64,8,2,128]{3,2,1,0:T(2,128)S(1)} %collective-permute-done.other_ref, ...), custom_call_target="tpu_custom_call", output_to_operand_aliasing={{0}: (3, {})} | custom-call | tf_op jit(solution)/shard_map/pallas_call | solution.py:253
Async XLA Ops:
  47.8 2.0 %copy-start = (s32[3]{0:T(128)S(1)}, s32[3]{0:T(128)}, u32[]{:S(2)}) copy-start(s32[3]{0:T(128)} %plan_ref.1) | copy-start | bytes 40
  47.8 3.6 %collective-permute-start = (f32[64,8,2,128]{3,2,1,0:T(2,128)S(1)}, f32[64,8,2,128]{3,2,1,0:T(2,128)S(1)}, u32[]{:S(2)}, u32[]{:S(2)}) collective-permute-start(f32[64,8,2,128]{3,2,1,0:T(2,128)S(1)} %bitcast.13), channel_id=1, source_target_pairs={{0,16},{16,0},{1,17},{17,1},{2,18},{18,2},{3,19},{19,3},{4,20},{20... | collective-permute-start | bytes 1572872 | tf_op jit(solution)/shard_map/ppermute | solution.py:234

commit v4 on v3

--- a/solution.py
+++ b/solution.py
@@ -15,6 +15,7 @@
 CARRIED = 16
 TILES = 4 * DATA // 8
 UPPER = 4
+FLIP = 0b101010
 SLOT = COLS // 8
 ROOM = pltpu.CompilerParams(vmem_limit_bytes=8 * 2**20)
 
@@ -220,7 +221,10 @@
     hbm = pl.BlockSpec(memory_space=pl.ANY)
     entries = grads.reshape(rows // 8, 8, tiles, COLS).transpose(0, 2, 1, 3)
     entries = entries.reshape(count, DATA // 2, 2, COLS)
-    arrived = lax.all_to_all(entries, EVERY, 0, 0, tiled=True)
+    arrived = lax.all_to_all(
+        entries, EVERY, 0, 0, tiled=True,
+        axis_index_groups=[[i ^ FLIP for i in range(count)]],
+    )
     peers = lax.axis_size(PLANE)
     share = pl.pallas_call(
         rounds,
@@ -229,7 +233,10 @@
         out_specs=vmem,
         compiler_params=ROOM,
     )(arrived.reshape(count // 4, 4 * DATA, COLS))
-    own = lax.all_to_all(share, PLANE, 0, 0, tiled=True)
+    own = lax.all_to_all(
+        share, PLANE, 0, 0, tiled=True,
+        axis_index_groups=[[i ^ FLIP for i in range(peers)]],
+    )
     own = own.reshape(peers, CARRIED // 2, 2, COLS)
     other = lax.ppermute(own, "core", [(0, 1), (1, 0)])
     whole_type = jax.ShapeDtypeStruct((count, DATA // 2, 2, COLS), jnp.float32)

time: 52.4 us -> 50.2 us (0.958)
  blocking collectives: 46.3 us -> 44.7 us
  starting transfers between devices: 2.01 us -> 1.47 us
    all_to_all x2, blocking collectives: 46.3 us -> 44.7 us  [the longest x1 29.3 us: on_device(): lax.all_to_all(entries, EVERY, 0, 0, tiled=True, axis_index_groups=[[i ^...]
    ppermute x1, starting transfers between devices: 2.01 us -> 1.47 us  [on_device(): other = lax.ppermute(own, 'core', [(0, 1), (1, 0)])]
where the time goes in v4:
time: 50.2 us; the launch traced here: 50 us
  blocking collectives  44.7 us (89%)
  Pallas kernels  2.54 us (5%)
  starting transfers between devices  1.47 us (3%)
  waiting for transfers between devices  0.71 us (1%)
  between operations  0.65 us (1%)
    all_to_all x1, blocking collectives, on_device(): lax.all_to_all(entries, EVERY, 0, 0, tiled=True, axis_index_groups=[[i ^...  29.3 us
    all_to_all x1, blocking collectives, on_device(): lax.all_to_all(share, PLANE, 0, 0, tiled=True, axis_index_groups=[[i ^ FL...  15.4 us
    ppermute x1, starting transfers between devices, on_device(): other = lax.ppermute(own, 'core', [(0, 1), (1, 0)])  1.47 us
  transfers between devices with their start and end apart: 1, of which 1 were waited for; matrix products, arithmetic and copies ran while one was open for 0% of the time, Pallas kernels for 2%

profile of v4, /device:TPU:1, one launch (start us, length us, event | category | flops | bytes accessed | tf_op | source)
XLA Modules:
  0.0 50.0 jit_solution(10427791927731243830)
XLA Ops:
  0.6 29.3 %all_to_all.10 = f32[128,7,2,128]{3,2,1,0:T(2,128)S(1)} all-to-all(f32[128,7,2,128]{3,2,1,0:T(2,128)} %bitcast.15), channel_id=1, replica_groups={{73,75,72,74,105,107,104,106,9,11,8,10,41,43,40,42,77,79,76,78,109,111,..., dimensions={0} | all-to-all | bytes 1835008 | tf_op jit(solution)/shard_map/all_to_all | solution.py:224
  29.9 0.9 %shard_map.41 = f32[64,16,128]{2,1,0:T(8,128)S(1)} custom-call(f32[32,56,128]{2,1,0:T(8,128)S(1)} %bitcast.12), custom_call_target="tpu_custom_call" | custom-call | tf_op jit(solution)/shard_map/pallas_call | solution.py:229
  30.8 15.4 %all_to_all.11 = f32[64,16,128]{2,1,0:T(8,128)S(1)} all-to-all(f32[64,16,128]{2,1,0:T(8,128)S(1)} %shard_map.41), channel_id=1, replica_groups={{73,75,72,74,105,107,104,106,9,11,8,10,41,43,40,42,77,79,76,78,109,111,..., dimensions={0} | all-to-all | bytes 1048576 | tf_op jit(solution)/shard_map/all_to_all | solution.py:236
  46.2 0.0 copy-start
  46.2 1.5 %collective-permute-start = (f32[64,8,2,128]{3,2,1,0:T(2,128)S(1)}, f32[64,8,2,128]{3,2,1,0:T(2,128)S(1)}, u32[]{:S(2)}, u32[]{:S(2)}) collective-permute-start(f32[64,8,2,128]{3,2,1,0:T(2,128)S(1)} %bitcast.13), channel_id=1, source_target_pairs={{0,16},{16,0},{1,17},{17,1},{2,18},{18,2},{3,19},{19,3},{4,20},{20... | collective-permute-start | bytes 1572872 | tf_op jit(solution)/shard_map/ppermute | solution.py:241
  47.6 0.0 copy-done
  47.7 0.8 %shard_map.42 = (f32[128,7,2,128]{3,2,1,0:T(2,128)}, f32[2,128]{1,0:T(2,128)S(1)}, f32[3,2,128]{2,1,0:T(2,128)S(1)}) custom-call(s32[3]{0:T(128)S(1)} %copy-done, f32[64,8,2,128]{3,2,1,0:T(2,128)S(1)} %bitcast.14), custom_call_target="tpu_custom_call" | custom-call | flops 10000000 | bytes 524288 | tf_op jit(solution)/shard_map/pallas_call | solution.py:247
  48.5 0.7 %collective-permute-done.other_ref = f32[64,8,2,128]{3,2,1,0:T(2,128)S(1)} collective-permute-done((f32[64,8,2,128]{3,2,1,0:T(2,128)S(1)}, f32[64,8,2,128]{3,2,1,0:T(2,128)S(1)}, u32[]{:S(2)}, u32[]{:S(2)}) %collective-permute-start) | collective-permute-done | bytes 524320 | tf_op jit(solution)/shard_map/ppermute | solution.py:241
  49.2 0.8 %shard_map.43 = (f32[128,7,2,128]{3,2,1,0:T(2,128)}, f32[3]{0:T(128)}) custom-call(f32[2,128]{1,0:T(2,128)S(1)} %get-tuple-element.7.worst_ref, f32[3,2,128]{2,1,0:T(2,128)S(1)} %get-tuple-element.8.asked_ref, f32[64,8,2,128]{3,2,1,0:T(2,128)S(1)} %collective-permute-done.other_ref, ...), custom_call_target="tpu_custom_call", output_to_operand_aliasing={{0}: (3, {})} | custom-call | tf_op jit(solution)/shard_map/pallas_call | solution.py:260
Async XLA Ops:
  46.2 1.5 %copy-start = (s32[3]{0:T(128)S(1)}, s32[3]{0:T(128)}, u32[]{:S(2)}) copy-start(s32[3]{0:T(128)} %plan_ref.1) | copy-start | bytes 40
  46.2 3.0 %collective-permute-start = (f32[64,8,2,128]{3,2,1,0:T(2,128)S(1)}, f32[64,8,2,128]{3,2,1,0:T(2,128)S(1)}, u32[]{:S(2)}, u32[]{:S(2)}) collective-permute-start(f32[64,8,2,128]{3,2,1,0:T(2,128)S(1)} %bitcast.13), channel_id=1, source_target_pairs={{0,16},{16,0},{1,17},{17,1},{2,18},{18,2},{3,19},{19,3},{4,20},{20... | collective-permute-start | bytes 1572872 | tf_op jit(solution)/shard_map/ppermute | solution.py:241

commit v5 on v3

v5 whole, which is shorter than its diff:
```python
import functools

import jax
import jax.numpy as jnp
from jax import lax
from jax.experimental import pallas as pl
from jax.experimental.pallas import tpu as pltpu
from jax.sharding import Mesh
from jax.sharding import PartitionSpec as P

PLANE = ("y", "z", "x_hi", "x_lo")
FLIP = 0b101010
COLS = 128
CHIP = 28
CORE = CHIP // 2
CARRIED = 16
SIDE = 2 * CHIP // 8
ONE = 4
SLOT = COLS // 8
ROOM = pltpu.CompilerParams(vmem_limit_bytes=8 * 2**20)


def both_ways(high, low, mean):
    return jnp.maximum(high - mean, mean - low)


def most(values):
    return functools.reduce(jnp.maximum, values)


def gaps(tiles, means):
    return [jnp.abs(t - m) for t, m in zip(tiles, means)]


def stats(values):
    return (
        functools.reduce(jnp.add, values),
        functools.reduce(jnp.maximum, values),
        functools.reduce(jnp.minimum, values),
    )


def halves(tiles):
    return [(a + b) * 0.5 for a, b in zip(tiles[:SIDE], tiles[SIDE:])]


def across_x_lo(tiles):
    turned = [pltpu.roll(t, 4, 0) for t in tiles]
    first = lax.broadcasted_iota(jnp.int32, (8, COLS), 0) < 4
    return [
        jnp.where(first, turned[(t + 3) % SIDE], turned[(t + 4) % SIDE])
        for t in range(SIDE)
    ]


def over_gy(tiles):
    other = across_x_lo(tiles[:SIDE]) + across_x_lo(tiles[SIDE:])
    return [(a + b) * 0.125 for a, b in zip(tiles, other)]


def tile(ref, i, t):
    return ref[i, 8 * t : 8 * t + 8]


def tiles_of(ref, i):
    return [tile(ref, i, t) for t in range(ref.shape[1] // 8)]


def put(ref, i, tiles):
    for t, value in enumerate(tiles):
        ref[i, 8 * t : 8 * t + 8] = value


def sums(g_ref, sum_ref):
    for y in range(4):
        put(
            sum_ref,
            y,
            [
                functools.reduce(
                    jnp.add, [tile(g_ref, 4 * y + z, t) for z in range(4)]
                )
                for t in range(2 * SIDE)
            ],
        )


def alone(
    g_ref, high_ref, low_ref, mz_high_ref, mz_low_ref, my_ref, myz_ref, far_ref
):
    dev_z, z_yz = [], []
    mz_of_z = [[] for _ in range(4)]
    for y in range(4):
        high, low, mz_high, mz_low = [], [], [], []
        for t in range(SIDE):
            mz = []
            for half in (t, t + SIDE):
                values = [tile(g_ref, 4 * y + z, half) for z in range(4)]
                _, top, bottom = stats(values)
                high.append(top)
                low.append(bottom)
            for z in range(4):
                a = tile(g_ref, 4 * y + z, t)
                mean = (a + tile(g_ref, 4 * y + z, t + SIDE)) * 0.5
                dev_z.append(jnp.abs(a - mean))
                mz.append(mean)
            _, top, bottom = stats(mz)
            mz_high.append(top)
            mz_low.append(bottom)
            dev_z = [most(dev_z)]
        put(high_ref, y, high[::2] + high[1::2])
        put(low_ref, y, low[::2] + low[1::2])
        put(mz_high_ref, y, mz_high)
        put(mz_low_ref, y, mz_low)

    dev_y, y_yz = [], []
    for z in range(4):
        found = [
            stats([tile(g_ref, 4 * y + z, t) for y in range(4)])
            for t in range(2 * SIDE)
        ]
        my = over_gy([f[0] for f in found])
        myz = halves(my)
        put(my_ref, z, my)
        put(myz_ref, z, myz)
        dev_y.append(most([both_ways(f[1], f[2], m) for f, m in zip(found, my)]))
        y_yz.append(most(gaps(my[:ONE], myz)))
        for t in range(SIDE):
            mz = [
                (tile(g_ref, 4 * y + z, t) + tile(g_ref, 4 * y + z, t + SIDE))
                * 0.5
                for y in range(4)
            ]
            _, top, bottom = stats(mz)
            z_yz.append(both_ways(top, bottom, myz[t]))
        z_yz = [most(z_yz)]
    for i, worst in enumerate((dev_y, dev_z, y_yz, z_yz)):
        far_ref[i] = most(worst)


def packed(eight):
    worst = jnp.concatenate(
        [jnp.max(v, axis=0, keepdims=True) for v in eight], axis=0
    )
    for apart in (64, 32, 16):
        worst = jnp.maximum(worst, pltpu.roll(worst, apart, 1))
    row = lax.broadcasted_iota(jnp.int32, worst.shape, 0)
    lane = lax.broadcasted_iota(jnp.int32, worst.shape, 1)
    return jnp.max(
        jnp.where(row == lane // SLOT, worst, 0.0), axis=0, keepdims=True
    )


def together(
    own_ref, other_ref, high_ref, low_ref, mz_high_ref, mz_low_ref, my_ref,
    myz_ref, far_ref, share_ref,
):
    mx, mxz, dev_x, z_xz = [], [], [], []
    for y in range(4):
        mx.append(
            [
                (a + b) * 0.125
                for a, b in zip(tiles_of(own_ref, y), tiles_of(other_ref, y))
            ]
        )
        mxz.append(halves(mx[y]))
        for t in range(2 * SIDE):
            dev_x.append(
                both_ways(tile(high_ref, y, t), tile(low_ref, y, t), mx[y][t])
            )
        for t in range(SIDE):
            z_xz.append(
                both_ways(
                    tile(mz_high_ref, y, t), tile(mz_low_ref, y, t), mxz[y][t]
                )
            )
        dev_x, z_xz = [most(dev_x)], [most(z_xz)]
    mxy = over_gy(
        [
            functools.reduce(jnp.add, [mx[y][t] for y in range(4)])
            for t in range(2 * SIDE)
        ]
    )
    mall = halves(mxy)
    once = (*range(ONE), *range(SIDE, SIDE + ONE))
    x_xy = most([most(gaps(mx[y], mxy)) for y in range(4)])
    x_xz = most([most(gaps(mx[y][:SIDE], mxz[y])) for y in range(4)])
    y_xy = most(
        [jnp.abs(tile(my_ref, z, t) - mxy[t]) for z in range(4) for t in once]
    )
    xy_all = most(gaps(mxy[:ONE], mall))
    xz_all = most([most(gaps(mxz[y], mall)) for y in range(4)])
    yz_all = most(
        [
            jnp.abs(tile(myz_ref, z, t) - mall[t])
            for z in range(4)
            for t in range(ONE)
        ]
    )
    none = jnp.zeros((8, COLS), jnp.float32)
    dev_y, dev_z, y_yz, z_yz = (far_ref[i] for i in range(4))
    slots = [dev_x[0], dev_y, dev_z]
    slots += [none, x_xy, x_xz, y_xy, none, y_yz]
    slots += [z_xz[0], z_yz, none]
    slots += [yz_all, xz_all, xy_all, none]
    mean = jnp.concatenate(mall[:ONE], axis=0)
    mine = jnp.where(
        lax.axis_index("core") == 0, mean[:CORE], mean[CORE : 2 * CORE]
    )
    share = jnp.concatenate([mine, packed(slots[:8]), packed(slots[8:])], axis=0)
    for i in range(share_ref.shape[0]):
        share_ref[i] = share


def begin(half_ref, out_ref, side, sems):
    count = half_ref.shape[0]
    part = count // sems.shape[0]
    copies = [
        pltpu.make_async_copy(
            half_ref.at[pl.ds(i * part, part), : CORE // 2],
            out_ref.at[pl.ds(i * part, part), side],
            sems.at[i],
        )
        for i in range(sems.shape[0])
    ]
    for copy in copies:
        copy.start()
    return copies


def put_own(
    plan_ref, own_ref, out_ref, worst_ref, asked_ref, plan_here, sems, plan_sem
):
    asked = pltpu.make_async_copy(plan_ref, plan_here, plan_sem)
    asked.start()
    copies = begin(own_ref, out_ref, lax.axis_index("core"), sems)
    worst = jnp.max(own_ref[:, CORE // 2], axis=0)
    worst_ref[...] = worst
    row = lax.broadcasted_iota(jnp.int32, worst.shape, 0)
    lane = lax.broadcasted_iota(jnp.int32, worst.shape, 1)
    slot = 8 * row + lane // SLOT
    asked.wait()
    a, b, c = plan_here[0], plan_here[1], plan_here[2]
    for r, wanted in enumerate((a, 3 + 3 * a + b, 12 + c)):
        asked_ref[r] = jnp.where(slot == wanted, 1.0, 0.0)
    for copy in copies:
        copy.wait()


def put_other(
    worst_ref, asked_ref, other_ref, _, out_ref, reports_ref,
    reports_here, sems, reports_sem,
):
    copies = begin(other_ref, out_ref, 1 - lax.axis_index("core"), sems)
    worst = jnp.maximum(
        worst_ref[...], jnp.max(other_ref[:, CORE // 2], axis=0)
    )
    for r in range(3):
        wanted = asked_ref[r] > 0.0
        reports_here[r] = jnp.max(jnp.where(wanted, worst, 0.0))
    told = pltpu.make_async_copy(reports_here, reports_ref, reports_sem)
    told.start()
    for copy in (*copies, told):
        copy.wait()


def on_device(grads, plan):
    rows, width = grads.shape[-2:]
    tiles = width // COLS
    chips = lax.axis_size(PLANE)
    real = functools.partial(jax.ShapeDtypeStruct, dtype=jnp.float32)
    vmem = pl.BlockSpec(memory_space=pltpu.VMEM)
    hbm = pl.BlockSpec(memory_space=pl.ANY)
    kernel = functools.partial(pl.pallas_call, compiler_params=ROOM)
    under_swap = pl.CostEstimate(
        flops=10**7, bytes_accessed=grads.size * 4, transcendentals=0
    )
    cores = [(0, 1), (1, 0)]
    members = [[i ^ FLIP for i in range(chips)]]

    entries = grads.reshape(rows // 8, 8, tiles, COLS).transpose(0, 2, 1, 3)
    entries = entries.reshape(chips, CHIP // 2, 2, COLS)
    arrived = lax.all_to_all(
        entries, PLANE, 0, 0, tiled=True, axis_index_groups=members
    ).reshape(chips // 4, 4 * CHIP, COLS)
    four, side = real((4, 4 * CHIP, COLS)), real((4, 2 * CHIP, COLS))
    own_sum = kernel(sums, out_shape=four, in_specs=[vmem], out_specs=vmem)(
        arrived
    )
    other_sum = lax.ppermute(own_sum, "core", cores)
    local = kernel(
        alone,
        out_shape=(four, four, side, side, four, side, real((4, 8, COLS))),
        in_specs=[vmem],
        out_specs=(vmem,) * 7,
        cost_estimate=under_swap,
    )(arrived)
    share = kernel(
        together,
        out_shape=real((chips, CARRIED, COLS)),
        in_specs=[vmem] * 9,
        out_specs=vmem,
    )(own_sum, other_sum, *local)
    own = lax.all_to_all(
        share, PLANE, 0, 0, tiled=True, axis_index_groups=members
    ).reshape(chips, CARRIED // 2, 2, COLS)
    other = lax.ppermute(own, "core", cores)
    whole = real((chips, 2, CORE // 2, 2, COLS))
    begun, worst, asked = kernel(
        put_own,
        out_shape=(whole, real((2, COLS)), real((3, 2, COLS))),
        in_specs=[hbm, vmem],
        out_specs=(hbm, vmem, vmem),
        scratch_shapes=[
            pltpu.SMEM(plan.shape, plan.dtype),
            pltpu.SemaphoreType.DMA((4,)),
            pltpu.SemaphoreType.DMA,
        ],
        cost_estimate=under_swap,
    )(plan, own)
    whole, reports = kernel(
        put_other,
        out_shape=(whole, real((3,))),
        in_specs=[vmem, vmem, vmem, hbm],
        out_specs=(hbm, hbm),
        scratch_shapes=[
            pltpu.SMEM((3,), jnp.float32),
            pltpu.SemaphoreType.DMA((4,)),
            pltpu.SemaphoreType.DMA,
        ],
        input_output_aliases={3: 0},
    )(worst, asked, other, begun)
    whole = whole.reshape(rows // 8, tiles, 8, COLS).transpose(0, 2, 1, 3)
    return whole.reshape(grads.shape), reports


def solution(mesh):
    torus = Mesh(
        mesh.devices.reshape(4, 2, 4, 2, mesh.shape["gz"]),
        ("z", "core", "y", "x_lo", "x_hi"),
    )
    placed = P(("z", "core"), ("y", "x_lo"), "x_hi", None, None)
    return jax.shard_map(
        on_device,
        mesh=torus,
        in_specs=(placed, P()),
        out_specs=(placed, P()),
        check_vma=False,
    )
```

time: 52.4 us -> 48.8 us (0.931)
  blocking collectives: 46.3 us -> 40.9 us
  starting transfers between devices: 2.01 us -> 3 us
  waiting for transfers between devices: 0.71 us -> 1.49 us
    all_to_all x2, blocking collectives: 46.3 us -> 40.9 us  [the longest x1 23.9 us: on_device(): lax.all_to_all(entries, PLANE, 0, 0, tiled=True, axis_index_groups=members)]
    ppermute x1 -> x2, starting transfers between devices: 2.01 us -> 3 us  [the longest x1 1.86 us: on_device(): other_sum = lax.ppermute(own_sum, 'core', cores)]
    ppermute x1 -> x2, waiting for transfers between devices: 0.71 us -> 1.49 us  [the longest x1 0.77 us: on_device(): other_sum = lax.ppermute(own_sum, 'core', cores)]
    pallas_call x3 -> x5, Pallas kernels: 2.54 us -> 2.46 us  [the longest x1 0.84 us: on_device(): kernel(put_other, out_shape=(whole, real((3,))), in_specs=[vmem, vmem, vm...]
  transfers between devices with their start and end apart: 1 -> 2, of which waited for: 1 -> 2; matrix products, arithmetic and copies ran while one was open for 0% -> 0% of each run, Pallas kernels for 2% -> 2%
where the time goes in v5:
time: 48.8 us; the launch traced here: 48.5 us
  blocking collectives  40.9 us (84%)
  starting transfers between devices  3 us (6%)
  Pallas kernels  2.46 us (5%)
  waiting for transfers between devices  1.49 us (3%)
  between operations  0.65 us (1%)
    all_to_all x1, blocking collectives, on_device(): lax.all_to_all(entries, PLANE, 0, 0, tiled=True, axis_index_groups=members)  23.9 us
    all_to_all x1, blocking collectives, on_device(): lax.all_to_all(share, PLANE, 0, 0, tiled=True, axis_index_groups=members)  17 us
    ppermute x1, starting transfers between devices, on_device(): other_sum = lax.ppermute(own_sum, 'core', cores)  1.86 us
    ppermute x1, starting transfers between devices, on_device(): other = lax.ppermute(own, 'core', cores)  1.14 us
  transfers between devices with their start and end apart: 2, of which 2 were waited for; matrix products, arithmetic and copies ran while one was open for 0% of the time, Pallas kernels for 2%

profile of v5, /device:TPU:1, one launch (start us, length us, event | category | flops | bytes accessed | tf_op | source)
XLA Modules:
  0.0 48.5 jit_solution(16967726751268062208)
XLA Ops:
  0.6 23.9 %all_to_all.10 = f32[64,14,2,128]{3,2,1,0:T(2,128)S(1)} all-to-all(f32[64,14,2,128]{3,2,1,0:T(2,128)} %bitcast.16), channel_id=1, replica_groups={{73,75,72,74,105,107,104,106,9,11,8,10,41,43,40,42,77,79,76,78,109,111,..., dimensions={0} | all-to-all | bytes 1835008 | tf_op jit(solution)/shard_map/all_to_all | solution.py:283
  24.6 1.9 %collective-permute-start = (f32[4,112,128]{2,1,0:T(8,128)S(1)}, f32[4,112,128]{2,1,0:T(8,128)S(1)}, u32[]{:S(2)}, u32[]{:S(2)}) collective-permute-start(f32[4,112,128]{2,1,0:T(8,128)S(1)} %shard_map.41.own_ref), channel_id=1, source_target_pairs={{0,16},{16,0},{1,17},{17,1},{2,18},{18,2},{3,19},{19,3},{4,20},{20... | collective-permute-start | bytes 688136 | tf_op jit(solution)/shard_map/ppermute | solution.py:290
  26.5 0.3 shard_map.42
  26.8 0.8 %collective-permute-done.other_ref = f32[4,112,128]{2,1,0:T(8,128)S(1)} collective-permute-done((f32[4,112,128]{2,1,0:T(8,128)S(1)}, f32[4,112,128]{2,1,0:T(8,128)S(1)}, u32[]{:S(2)}, u32[]{:S(2)}) %collective-permute-start) | collective-permute-done | bytes 229408 | tf_op jit(solution)/shard_map/ppermute | solution.py:290
  27.6 0.4 shard_map.43
  28.0 17.0 %all_to_all.11 = f32[64,16,128]{2,1,0:T(8,128)S(1)} all-to-all(f32[64,16,128]{2,1,0:T(8,128)S(1)} %shard_map.43), channel_id=1, replica_groups={{73,75,72,74,105,107,104,106,9,11,8,10,41,43,40,42,77,79,76,78,109,111,..., dimensions={0} | all-to-all | bytes 1048576 | tf_op jit(solution)/shard_map/all_to_all | solution.py:304
  45.0 0.0 copy-start
  45.0 1.1 %collective-permute-start.1 = (f32[64,8,2,128]{3,2,1,0:T(2,128)S(1)}, f32[64,8,2,128]{3,2,1,0:T(2,128)S(1)}, u32[]{:S(2)}, u32[]{:S(2)}) collective-permute-start(f32[64,8,2,128]{3,2,1,0:T(2,128)S(1)} %bitcast.14), channel_id=1, source_target_pairs={{0,16},{16,0},{1,17},{17,1},{2,18},{18,2},{3,19},{19,3},{4,20},{20... | collective-permute-start | bytes 1572872 | tf_op jit(solution)/shard_map/ppermute | solution.py:307
  46.1 0.0 copy-done
  46.2 0.8 %shard_map.44 = (f32[64,2,7,2,128]{4,3,2,1,0:T(2,128)}, f32[2,128]{1,0:T(2,128)S(1)}, f32[3,2,128]{2,1,0:T(2,128)S(1)}) custom-call(s32[3]{0:T(128)S(1)} %copy-done, f32[64,8,2,128]{3,2,1,0:T(2,128)S(1)} %bitcast.15), custom_call_target="tpu_custom_call" | custom-call | flops 10000000 | bytes 917504 | tf_op jit(solution)/shard_map/pallas_call | solution.py:309
  47.0 0.7 %collective-permute-done.1.other_ref = f32[64,8,2,128]{3,2,1,0:T(2,128)S(1)} collective-permute-done((f32[64,8,2,128]{3,2,1,0:T(2,128)S(1)}, f32[64,8,2,128]{3,2,1,0:T(2,128)S(1)}, u32[]{:S(2)}, u32[]{:S(2)}) %collective-permute-start.1) | collective-permute-done | bytes 524320 | tf_op jit(solution)/shard_map/ppermute | solution.py:307
  47.7 0.8 %shard_map.45 = (f32[64,2,7,2,128]{4,3,2,1,0:T(2,128)}, f32[3]{0:T(128)}) custom-call(f32[2,128]{1,0:T(2,128)S(1)} %get-tuple-element.21.worst_ref, f32[3,2,128]{2,1,0:T(2,128)S(1)} %get-tuple-element.22.asked_ref, f32[64,8,2,128]{3,2,1,0:T(2,128)S(1)} %collective-permute-done.1.other_ref, ...), custom_call_target="tpu_custom_call", output_to_operand_aliasing={{0}: (3, {})} | custom-call | tf_op jit(solution)/shard_map/pallas_call | solution.py:321
  (1 shorter events, 0.0 us)
Async XLA Ops:
  24.6 3.0 %collective-permute-start = (f32[4,112,128]{2,1,0:T(8,128)S(1)}, f32[4,112,128]{2,1,0:T(8,128)S(1)}, u32[]{:S(2)}, u32[]{:S(2)}) collective-permute-start(f32[4,112,128]{2,1,0:T(8,128)S(1)} %shard_map.41.own_ref), channel_id=1, source_target_pairs={{0,16},{16,0},{1,17},{17,1},{2,18},{18,2},{3,19},{19,3},{4,20},{20... | collective-permute-start | bytes 688136 | tf_op jit(solution)/shard_map/ppermute | solution.py:290
  45.0 1.1 %copy-start = (s32[3]{0:T(128)S(1)}, s32[3]{0:T(128)}, u32[]{:S(2)}) copy-start(s32[3]{0:T(128)} %plan_ref.1) | copy-start | bytes 40
  45.0 2.7 %collective-permute-start.1 = (f32[64,8,2,128]{3,2,1,0:T(2,128)S(1)}, f32[64,8,2,128]{3,2,1,0:T(2,128)S(1)}, u32[]{:S(2)}, u32[]{:S(2)}) collective-permute-start(f32[64,8,2,128]{3,2,1,0:T(2,128)S(1)} %bitcast.14), channel_id=1, source_target_pairs={{0,16},{16,0},{1,17},{17,1},{2,18},{18,2},{3,19},{19,3},{4,20},{20... | collective-permute-start | bytes 1572872 | tf_op jit(solution)/shard_map/ppermute | solution.py:307

commit v6 on v5

--- a/solution.py
+++ b/solution.py
@@ -9,14 +9,13 @@
 from jax.sharding import PartitionSpec as P
 
 PLANE = ("y", "z", "x_hi", "x_lo")
-FLIP = 0b101010
+YZ_ORDER, X_ORDER = (2, 0, 1, 3), (2, 3, 0, 1)
 COLS = 128
 CHIP = 28
 CORE = CHIP // 2
 CARRIED = 16
 SIDE = 2 * CHIP // 8
 ONE = 4
-SLOT = COLS // 8
 ROOM = pltpu.CompilerParams(vmem_limit_bytes=8 * 2**20)
 
 
@@ -86,8 +85,11 @@
 
 
 def alone(
-    g_ref, high_ref, low_ref, mz_high_ref, mz_low_ref, my_ref, myz_ref, far_ref
+    plan_ref, g_ref, high_ref, low_ref, mz_high_ref, mz_low_ref, my_ref,
+    myz_ref, far_ref, mask_ref, plan_here, plan_sem,
 ):
+    asked = pltpu.make_async_copy(plan_ref, plan_here, plan_sem)
+    asked.start()
     dev_z, z_yz = [], []
     mz_of_z = [[] for _ in range(4)]
     for y in range(4):
@@ -136,24 +138,28 @@
         z_yz = [most(z_yz)]
     for i, worst in enumerate((dev_y, dev_z, y_yz, z_yz)):
         far_ref[i] = most(worst)
-
-
-def packed(eight):
-    worst = jnp.concatenate(
-        [jnp.max(v, axis=0, keepdims=True) for v in eight], axis=0
-    )
-    for apart in (64, 32, 16):
-        worst = jnp.maximum(worst, pltpu.roll(worst, apart, 1))
-    row = lax.broadcasted_iota(jnp.int32, worst.shape, 0)
-    lane = lax.broadcasted_iota(jnp.int32, worst.shape, 1)
-    return jnp.max(
-        jnp.where(row == lane // SLOT, worst, 0.0), axis=0, keepdims=True
-    )
+    asked.wait()
+    wanted(plan_here, mask_ref)
+
+
+def wanted(plan_ref, mask_ref):
+    a, b, c = plan_ref[0], plan_ref[1], plan_ref[2]
+    for i in range(mask_ref.shape[0]):
+        asked = (i == a) | (i == 3 + 3 * a + b) | (i == 12 + c)
+        mask_ref[i] = jnp.full((8, COLS), jnp.where(asked, 1.0, 0.0))
+
+
+def folded(mask_ref, choices):
+    worst = most(
+        [jnp.where(mask_ref[i] > 0.0, v, 0.0) for i, v in choices.items()]
+    )
+    worst = jnp.max(worst, axis=0, keepdims=True)
+    return jnp.maximum(worst, pltpu.roll(worst, COLS // 2, 1))
 
 
 def together(
     own_ref, other_ref, high_ref, low_ref, mz_high_ref, mz_low_ref, my_ref,
-    myz_ref, far_ref, share_ref,
+    myz_ref, far_ref, mask_ref, share_ref,
 ):
     mx, mxz, dev_x, z_xz = [], [], [], []
     for y in range(4):
@@ -197,17 +203,20 @@
             for t in range(ONE)
         ]
     )
-    none = jnp.zeros((8, COLS), jnp.float32)
     dev_y, dev_z, y_yz, z_yz = (far_ref[i] for i in range(4))
-    slots = [dev_x[0], dev_y, dev_z]
-    slots += [none, x_xy, x_xz, y_xy, none, y_yz]
-    slots += [z_xz[0], z_yz, none]
-    slots += [yz_all, xz_all, xy_all, none]
+    first = folded(mask_ref, {0: dev_x[0], 1: dev_y, 2: dev_z})
+    second = folded(
+        mask_ref,
+        {4: x_xy, 5: x_xz, 6: y_xy, 8: y_yz, 9: z_xz[0], 10: z_yz},
+    )
+    third = folded(mask_ref, {12: yz_all, 13: xz_all, 14: xy_all})
+    lane = lax.broadcasted_iota(jnp.int32, (1, COLS), 1)
+    told = [jnp.where(lane < COLS // 2, first, second), third]
     mean = jnp.concatenate(mall[:ONE], axis=0)
     mine = jnp.where(
         lax.axis_index("core") == 0, mean[:CORE], mean[CORE : 2 * CORE]
     )
-    share = jnp.concatenate([mine, packed(slots[:8]), packed(slots[8:])], axis=0)
+    share = jnp.concatenate([mine, *told], axis=0)
     for i in range(share_ref.shape[0]):
         share_ref[i] = share
 
@@ -228,36 +237,26 @@
     return copies
 
 
-def put_own(
-    plan_ref, own_ref, out_ref, worst_ref, asked_ref, plan_here, sems, plan_sem
-):
-    asked = pltpu.make_async_copy(plan_ref, plan_here, plan_sem)
-    asked.start()
+def put_own(own_ref, out_ref, worst_ref, sems):
     copies = begin(own_ref, out_ref, lax.axis_index("core"), sems)
-    worst = jnp.max(own_ref[:, CORE // 2], axis=0)
-    worst_ref[...] = worst
-    row = lax.broadcasted_iota(jnp.int32, worst.shape, 0)
-    lane = lax.broadcasted_iota(jnp.int32, worst.shape, 1)
-    slot = 8 * row + lane // SLOT
-    asked.wait()
-    a, b, c = plan_here[0], plan_here[1], plan_here[2]
-    for r, wanted in enumerate((a, 3 + 3 * a + b, 12 + c)):
-        asked_ref[r] = jnp.where(slot == wanted, 1.0, 0.0)
+    worst_ref[...] = jnp.max(own_ref[:, CORE // 2], axis=0)
     for copy in copies:
         copy.wait()
 
 
 def put_other(
-    worst_ref, asked_ref, other_ref, _, out_ref, reports_ref,
+    worst_ref, other_ref, _, out_ref, reports_ref,
     reports_here, sems, reports_sem,
 ):
     copies = begin(other_ref, out_ref, 1 - lax.axis_index("core"), sems)
     worst = jnp.maximum(
         worst_ref[...], jnp.max(other_ref[:, CORE // 2], axis=0)
     )
-    for r in range(3):
-        wanted = asked_ref[r] > 0.0
-        reports_here[r] = jnp.max(jnp.where(wanted, worst, 0.0))
+    lane = lax.broadcasted_iota(jnp.int32, (1, COLS), 1)
+    first = lane < COLS // 2
+    reports_here[0] = jnp.max(jnp.where(first, worst[:1], 0.0))
+    reports_here[1] = jnp.max(jnp.where(first, 0.0, worst[:1]))
+    reports_here[2] = jnp.max(worst[1:])
     told = pltpu.make_async_copy(reports_here, reports_ref, reports_sem)
     told.start()
     for copy in (*copies, told):
@@ -276,7 +275,9 @@
         flops=10**7, bytes_accessed=grads.size * 4, transcendentals=0
     )
     cores = [(0, 1), (1, 0)]
-    members = [[i ^ FLIP for i in range(chips)]]
+    members = [
+        [16 * y + 4 * z + x for y in YZ_ORDER for z in YZ_ORDER for x in X_ORDER]
+    ]
 
     entries = grads.reshape(rows // 8, 8, tiles, COLS).transpose(0, 2, 1, 3)
     entries = entries.reshape(chips, CHIP // 2, 2, COLS)
@@ -290,15 +291,23 @@
     other_sum = lax.ppermute(own_sum, "core", cores)
     local = kernel(
         alone,
-        out_shape=(four, four, side, side, four, side, real((4, 8, COLS))),
-        in_specs=[vmem],
-        out_specs=(vmem,) * 7,
+        out_shape=(
+            *(four, four, side, side, four, side),
+            real((4, 8, COLS)),
+            real((15, 8, COLS)),
+        ),
+        in_specs=[hbm, vmem],
+        out_specs=(vmem,) * 8,
+        scratch_shapes=[
+            pltpu.SMEM(plan.shape, plan.dtype),
+            pltpu.SemaphoreType.DMA,
+        ],
         cost_estimate=under_swap,
-    )(arrived)
+    )(plan, arrived)
     share = kernel(
         together,
         out_shape=real((chips, CARRIED, COLS)),
-        in_specs=[vmem] * 9,
+        in_specs=[vmem] * 10,
         out_specs=vmem,
     )(own_sum, other_sum, *local)
     own = lax.all_to_all(
@@ -306,30 +315,26 @@
     ).reshape(chips, CARRIED // 2, 2, COLS)
     other = lax.ppermute(own, "core", cores)
     whole = real((chips, 2, CORE // 2, 2, COLS))
-    begun, worst, asked = kernel(
+    begun, worst = kernel(
         put_own,
-        out_shape=(whole, real((2, COLS)), real((3, 2, COLS))),
-        in_specs=[hbm, vmem],
-        out_specs=(hbm, vmem, vmem),
-        scratch_shapes=[
-            pltpu.SMEM(plan.shape, plan.dtype),
-            pltpu.SemaphoreType.DMA((4,)),
-            pltpu.SemaphoreType.DMA,
-        ],
+        out_shape=(whole, real((2, COLS))),
+        in_specs=[vmem],
+        out_specs=(hbm, vmem),
+        scratch_shapes=[pltpu.SemaphoreType.DMA((2,))],
         cost_estimate=under_swap,
-    )(plan, own)
+    )(own)
     whole, reports = kernel(
         put_other,
         out_shape=(whole, real((3,))),
-        in_specs=[vmem, vmem, vmem, hbm],
+        in_specs=[vmem, vmem, hbm],
         out_specs=(hbm, hbm),
         scratch_shapes=[
             pltpu.SMEM((3,), jnp.float32),
-            pltpu.SemaphoreType.DMA((4,)),
+            pltpu.SemaphoreType.DMA((2,)),
             pltpu.SemaphoreType.DMA,
         ],
-        input_output_aliases={3: 0},
-    )(worst, asked, other, begun)
+        input_output_aliases={2: 0},
+    )(worst, other, begun)
     whole = whole.reshape(rows // 8, tiles, 8, COLS).transpose(0, 2, 1, 3)
     return whole.reshape(grads.shape), reports
 

time: 48.8 us -> 48.2 us (0.988)
  blocking collectives: 40.9 us -> 40.1 us
    all_to_all x1, blocking collectives: 17 us -> 15.8 us  [on_device(): lax.all_to_all(share, PLANE, 0, 0, tiled=True, axis_index_groups=members)]
  transfers between devices with their start and end apart: 2 -> 2, of which waited for: 2 -> 2; matrix products, arithmetic and copies ran while one was open for 0% -> 0% of each run, Pallas kernels for 2% -> 3%
where the time goes in v6:
time: 48.2 us; the launch traced here: 47.9 us
  blocking collectives  40.1 us (83%)
  starting transfers between devices  3.32 us (7%)
  Pallas kernels  2.53 us (5%)
  waiting for transfers between devices  1.26 us (3%)
  between operations  0.66 us (1%)
    all_to_all x1, blocking collectives, on_device(): lax.all_to_all(entries, PLANE, 0, 0, tiled=True, axis_index_groups=members)  24.3 us
    all_to_all x1, blocking collectives, on_device(): lax.all_to_all(share, PLANE, 0, 0, tiled=True, axis_index_groups=members)  15.8 us
    ppermute x1, starting transfers between devices, on_device(): other_sum = lax.ppermute(own_sum, 'core', cores)  1.7 us
    ppermute x1, starting transfers between devices, on_device(): other = lax.ppermute(own, 'core', cores)  1.62 us
  transfers between devices with their start and end apart: 2, of which 2 were waited for; matrix products, arithmetic and copies ran while one was open for 0% of the time, Pallas kernels for 3%

profile of v6, /device:TPU:1, one launch (start us, length us, event | category | flops | bytes accessed | tf_op | source)
XLA Modules:
  0.0 47.9 jit_solution(15189234991566970993)
XLA Ops:
  0.6 24.3 %all_to_all.10 = f32[64,14,2,128]{3,2,1,0:T(2,128)S(1)} all-to-all(f32[64,14,2,128]{3,2,1,0:T(2,128)} %bitcast.16), channel_id=1, replica_groups={{73,75,72,74,9,11,8,10,41,43,40,42,105,107,104,106,65,67,64,66,1,3,0,2,..., dimensions={0} | all-to-all | bytes 1835008 | tf_op jit(solution)/shard_map/all_to_all | solution.py:284
  24.9 0.0 copy-start
  25.0 1.7 %collective-permute-start = (f32[4,112,128]{2,1,0:T(8,128)S(1)}, f32[4,112,128]{2,1,0:T(8,128)S(1)}, u32[]{:S(2)}, u32[]{:S(2)}) collective-permute-start(f32[4,112,128]{2,1,0:T(8,128)S(1)} %shard_map.41.own_ref), channel_id=1, source_target_pairs={{0,16},{16,0},{1,17},{17,1},{2,18},{18,2},{3,19},{19,3},{4,20},{20... | collective-permute-start | bytes 688136 | tf_op jit(solution)/shard_map/ppermute | solution.py:291
  26.7 0.0 copy-done
  26.7 0.6 %shard_map.42 = (f32[4,112,128]{2,1,0:T(8,128)S(1)}, f32[4,112,128]{2,1,0:T(8,128)S(1)}, f32[4,56,128]{2,1,0:T(8,128)S(1)}, f32[4,56,128]{2,1,0:T(8,128)S(1)}, f...) custom-call(s32[3]{0:T(128)S(1)} %copy-done, ...), custom_call_target="tpu_custom_call" | custom-call | flops 10000000 | bytes 917504 | tf_op jit(solution)/shard_map/pallas_call | solution.py:292
  27.2 0.5 %collective-permute-done.other_ref = f32[4,112,128]{2,1,0:T(8,128)S(1)} collective-permute-done((f32[4,112,128]{2,1,0:T(8,128)S(1)}, f32[4,112,128]{2,1,0:T(8,128)S(1)}, u32[]{:S(2)}, u32[]{:S(2)}) %collective-permute-start) | collective-permute-done | bytes 229408 | tf_op jit(solution)/shard_map/ppermute | solution.py:291
  27.8 0.3 shard_map.43
  28.1 15.8 %all_to_all.11 = f32[64,16,128]{2,1,0:T(8,128)S(1)} all-to-all(f32[64,16,128]{2,1,0:T(8,128)S(1)} %shard_map.43), channel_id=1, replica_groups={{73,75,72,74,9,11,8,10,41,43,40,42,105,107,104,106,65,67,64,66,1,3,0,2,..., dimensions={0} | all-to-all | bytes 1048576 | tf_op jit(solution)/shard_map/all_to_all | solution.py:313
  43.9 1.6 %collective-permute-start.1 = (f32[64,8,2,128]{3,2,1,0:T(2,128)S(1)}, f32[64,8,2,128]{3,2,1,0:T(2,128)S(1)}, u32[]{:S(2)}, u32[]{:S(2)}) collective-permute-start(f32[64,8,2,128]{3,2,1,0:T(2,128)S(1)} %bitcast.14), channel_id=1, source_target_pairs={{0,16},{16,0},{1,17},{17,1},{2,18},{18,2},{3,19},{19,3},{4,20},{20... | collective-permute-start | bytes 1572872 | tf_op jit(solution)/shard_map/ppermute | solution.py:316
  45.5 0.8 %shard_map.44 = (f32[64,2,7,2,128]{4,3,2,1,0:T(2,128)}, f32[2,128]{1,0:T(2,128)S(1)}) custom-call(f32[64,8,2,128]{3,2,1,0:T(2,128)S(1)} %bitcast.15), custom_call_target="tpu_custom_call" | custom-call | flops 10000000 | bytes 917504 | tf_op jit(solution)/shard_map/pallas_call | solution.py:318
  46.3 0.7 %collective-permute-done.1.other_ref = f32[64,8,2,128]{3,2,1,0:T(2,128)S(1)} collective-permute-done((f32[64,8,2,128]{3,2,1,0:T(2,128)S(1)}, f32[64,8,2,128]{3,2,1,0:T(2,128)S(1)}, u32[]{:S(2)}, u32[]{:S(2)}) %collective-permute-start.1) | collective-permute-done | bytes 524320 | tf_op jit(solution)/shard_map/ppermute | solution.py:316
  47.1 0.8 %shard_map.45 = (f32[64,2,7,2,128]{4,3,2,1,0:T(2,128)}, f32[3]{0:T(128)}) custom-call(f32[2,128]{1,0:T(2,128)S(1)} %get-tuple-element.22.worst_ref, f32[64,8,2,128]{3,2,1,0:T(2,128)S(1)} %collective-permute-done.1.other_ref, f32[64,2,7,2,128]{4,3,2,1,0:T(2,128)} %get-tuple-element.23._), custom_call_target="tpu_custom_call", output_to_operand_aliasing={{0}: (2, {})} | custom-call | tf_op jit(solution)/shard_map/pallas_call | solution.py:326
  (1 shorter events, 0.0 us)
Async XLA Ops:
  24.9 1.8 %copy-start = (s32[3]{0:T(128)S(1)}, s32[3]{0:T(128)}, u32[]{:S(2)}) copy-start(s32[3]{0:T(128)} %plan_ref.1) | copy-start | bytes 40
  25.0 2.8 %collective-permute-start = (f32[4,112,128]{2,1,0:T(8,128)S(1)}, f32[4,112,128]{2,1,0:T(8,128)S(1)}, u32[]{:S(2)}, u32[]{:S(2)}) collective-permute-start(f32[4,112,128]{2,1,0:T(8,128)S(1)} %shard_map.41.own_ref), channel_id=1, source_target_pairs={{0,16},{16,0},{1,17},{17,1},{2,18},{18,2},{3,19},{19,3},{4,20},{20... | collective-permute-start | bytes 688136 | tf_op jit(solution)/shard_map/ppermute | solution.py:291
  43.9 3.2 %collective-permute-start.1 = (f32[64,8,2,128]{3,2,1,0:T(2,128)S(1)}, f32[64,8,2,128]{3,2,1,0:T(2,128)S(1)}, u32[]{:S(2)}, u32[]{:S(2)}) collective-permute-start(f32[64,8,2,128]{3,2,1,0:T(2,128)S(1)} %bitcast.14), channel_id=1, source_target_pairs={{0,16},{16,0},{1,17},{17,1},{2,18},{18,2},{3,19},{19,3},{4,20},{20... | collective-permute-start | bytes 1572872 | tf_op jit(solution)/shard_map/ppermute | solution.py:316

commit v7 on v6

--- a/solution.py
+++ b/solution.py
@@ -8,7 +8,7 @@
 from jax.sharding import Mesh
 from jax.sharding import PartitionSpec as P
 
-PLANE = ("y", "z", "x_hi", "x_lo")
+PLANE = ("z", "y", "x_hi", "x_lo")
 YZ_ORDER, X_ORDER = (2, 0, 1, 3), (2, 3, 0, 1)
 COLS = 128
 CHIP = 28
@@ -77,7 +77,7 @@
             y,
             [
                 functools.reduce(
-                    jnp.add, [tile(g_ref, 4 * y + z, t) for z in range(4)]
+                    jnp.add, [tile(g_ref, 4 * z + y, t) for z in range(4)]
                 )
                 for t in range(2 * SIDE)
             ],
@@ -85,11 +85,8 @@
 
 
 def alone(
-    plan_ref, g_ref, high_ref, low_ref, mz_high_ref, mz_low_ref, my_ref,
-    myz_ref, far_ref, mask_ref, plan_here, plan_sem,
+    g_ref, high_ref, low_ref, mz_high_ref, mz_low_ref, my_ref, myz_ref, far_ref
 ):
-    asked = pltpu.make_async_copy(plan_ref, plan_here, plan_sem)
-    asked.start()
     dev_z, z_yz = [], []
     mz_of_z = [[] for _ in range(4)]
     for y in range(4):
@@ -97,13 +94,13 @@
         for t in range(SIDE):
             mz = []
             for half in (t, t + SIDE):
-                values = [tile(g_ref, 4 * y + z, half) for z in range(4)]
+                values = [tile(g_ref, 4 * z + y, half) for z in range(4)]
                 _, top, bottom = stats(values)
                 high.append(top)
                 low.append(bottom)
             for z in range(4):
-                a = tile(g_ref, 4 * y + z, t)
-                mean = (a + tile(g_ref, 4 * y + z, t + SIDE)) * 0.5
+                a = tile(g_ref, 4 * z + y, t)
+                mean = (a + tile(g_ref, 4 * z + y, t + SIDE)) * 0.5
                 dev_z.append(jnp.abs(a - mean))
                 mz.append(mean)
             _, top, bottom = stats(mz)
@@ -118,7 +115,7 @@
     dev_y, y_yz = [], []
     for z in range(4):
         found = [
-            stats([tile(g_ref, 4 * y + z, t) for y in range(4)])
+            stats([tile(g_ref, 4 * z + y, t) for y in range(4)])
             for t in range(2 * SIDE)
         ]
         my = over_gy([f[0] for f in found])
@@ -129,7 +126,7 @@
         y_yz.append(most(gaps(my[:ONE], myz)))
         for t in range(SIDE):
             mz = [
-                (tile(g_ref, 4 * y + z, t) + tile(g_ref, 4 * y + z, t + SIDE))
+                (tile(g_ref, 4 * z + y, t) + tile(g_ref, 4 * z + y, t + SIDE))
                 * 0.5
                 for y in range(4)
             ]
@@ -138,12 +135,13 @@
         z_yz = [most(z_yz)]
     for i, worst in enumerate((dev_y, dev_z, y_yz, z_yz)):
         far_ref[i] = most(worst)
+
+
+def wanted(plan_ref, mask_ref, plan_here, plan_sem):
+    asked = pltpu.make_async_copy(plan_ref, plan_here, plan_sem)
+    asked.start()
     asked.wait()
-    wanted(plan_here, mask_ref)
-
-
-def wanted(plan_ref, mask_ref):
-    a, b, c = plan_ref[0], plan_ref[1], plan_ref[2]
+    a, b, c = plan_here[0], plan_here[1], plan_here[2]
     for i in range(mask_ref.shape[0]):
         asked = (i == a) | (i == 3 + 3 * a + b) | (i == 12 + c)
         mask_ref[i] = jnp.full((8, COLS), jnp.where(asked, 1.0, 0.0))
@@ -276,7 +274,7 @@
     )
     cores = [(0, 1), (1, 0)]
     members = [
-        [16 * y + 4 * z + x for y in YZ_ORDER for z in YZ_ORDER for x in X_ORDER]
+        [16 * z + 4 * y + x for z in YZ_ORDER for y in YZ_ORDER for x in X_ORDER]
     ]
 
     entries = grads.reshape(rows // 8, 8, tiles, COLS).transpose(0, 2, 1, 3)
@@ -294,22 +292,28 @@
         out_shape=(
             *(four, four, side, side, four, side),
             real((4, 8, COLS)),
-            real((15, 8, COLS)),
         ),
-        in_specs=[hbm, vmem],
-        out_specs=(vmem,) * 8,
+        in_specs=[vmem],
+        out_specs=(vmem,) * 7,
+        cost_estimate=under_swap,
+    )(arrived)
+    mask = kernel(
+        wanted,
+        out_shape=real((15, 8, COLS)),
+        in_specs=[hbm],
+        out_specs=vmem,
         scratch_shapes=[
             pltpu.SMEM(plan.shape, plan.dtype),
             pltpu.SemaphoreType.DMA,
         ],
         cost_estimate=under_swap,
-    )(plan, arrived)
+    )(plan)
     share = kernel(
         together,
         out_shape=real((chips, CARRIED, COLS)),
         in_specs=[vmem] * 10,
         out_specs=vmem,
-    )(own_sum, other_sum, *local)
+    )(own_sum, other_sum, *local, mask)
     own = lax.all_to_all(
         share, PLANE, 0, 0, tiled=True, axis_index_groups=members
     ).reshape(chips, CARRIED // 2, 2, COLS)

time: 48.2 us -> 48.1 us (level)
  starting transfers between devices: 3.32 us -> 2.2 us
  blocking collectives: 40.1 us -> 41.2 us
    ppermute x1, starting transfers between devices: 1.7 us -> 0.6 us  [on_device(): other_sum = lax.ppermute(own_sum, 'core', cores)]
    all_to_all x1, blocking collectives: 24.3 us -> 25.2 us  [on_device(): lax.all_to_all(entries, PLANE, 0, 0, tiled=True, axis_index_groups=members)]
    pallas_call x0 -> x1, Pallas kernels: none -> 0.58 us  [on_device(): kernel(wanted, out_shape=real((15, 8, COLS)), in_specs=[hbm], out_specs=v...]
  transfers between devices with their start and end apart: 2 -> 2, of which waited for: 2 -> 2; matrix products, arithmetic and copies ran while one was open for 0% -> 0% of each run, Pallas kernels for 3% -> 4%
where the time goes in v7:
time: 48.1 us; the launch traced here: 47.8 us
  blocking collectives  41.2 us (86%)
  Pallas kernels  2.87 us (6%)
  starting transfers between devices  2.2 us (5%)
  waiting for transfers between devices  0.91 us (2%)
  between operations  0.66 us (1%)
    all_to_all x1, blocking collectives, on_device(): lax.all_to_all(entries, PLANE, 0, 0, tiled=True, axis_index_groups=members)  25.2 us
    all_to_all x1, blocking collectives, on_device(): lax.all_to_all(share, PLANE, 0, 0, tiled=True, axis_index_groups=members)  16 us
    ppermute x1, starting transfers between devices, on_device(): other = lax.ppermute(own, 'core', cores)  1.6 us
  transfers between devices with their start and end apart: 2, of which 2 were waited for; matrix products, arithmetic and copies ran while one was open for 0% of the time, Pallas kernels for 4%

profile of v7, /device:TPU:1, one launch (start us, length us, event | category | flops | bytes accessed | tf_op | source)
XLA Modules:
  0.0 47.8 jit_solution(2315076090638222184)
XLA Ops:
  0.6 25.2 %all_to_all.10 = f32[64,14,2,128]{3,2,1,0:T(2,128)S(1)} all-to-all(f32[64,14,2,128]{3,2,1,0:T(2,128)} %bitcast.16), channel_id=1, replica_groups={{73,75,72,74,65,67,64,66,69,71,68,70,77,79,76,78,9,11,8,10,1,3,0,2,5,7,..., dimensions={0} | all-to-all | bytes 1835008 | tf_op jit(solution)/shard_map/all_to_all | solution.py:282
  25.8 0.0 copy-start
  25.9 0.6 %collective-permute-start = (f32[4,112,128]{2,1,0:T(8,128)S(1)}, f32[4,112,128]{2,1,0:T(8,128)S(1)}, u32[]{:S(2)}, u32[]{:S(2)}) collective-permute-start(f32[4,112,128]{2,1,0:T(8,128)S(1)} %shard_map.41.own_ref), channel_id=1, source_target_pairs={{0,16},{16,0},{1,17},{17,1},{2,18},{18,2},{3,19},{19,3},{4,20},{20... | collective-permute-start | bytes 688136 | tf_op jit(solution)/shard_map/ppermute | solution.py:289
  26.5 0.0 copy-done
  26.5 0.6 %shard_map.43.mask_ref = f32[15,8,128]{2,1,0:T(8,128)S(1)} custom-call(s32[3]{0:T(128)S(1)} %copy-done), custom_call_target="tpu_custom_call" | custom-call | flops 10000000 | bytes 917504 | tf_op jit(solution)/shard_map/pallas_call | solution.py:300
  27.1 0.3 shard_map.42
  27.4 0.2 collective-permute-done.other_ref
  27.6 0.3 shard_map.44
  27.9 16.0 %all_to_all.11 = f32[64,16,128]{2,1,0:T(8,128)S(1)} all-to-all(f32[64,16,128]{2,1,0:T(8,128)S(1)} %shard_map.44), channel_id=1, replica_groups={{73,75,72,74,65,67,64,66,69,71,68,70,77,79,76,78,9,11,8,10,1,3,0,2,5,7,..., dimensions={0} | all-to-all | bytes 1048576 | tf_op jit(solution)/shard_map/all_to_all | solution.py:317
  43.9 1.6 %collective-permute-start.1 = (f32[64,8,2,128]{3,2,1,0:T(2,128)S(1)}, f32[64,8,2,128]{3,2,1,0:T(2,128)S(1)}, u32[]{:S(2)}, u32[]{:S(2)}) collective-permute-start(f32[64,8,2,128]{3,2,1,0:T(2,128)S(1)} %bitcast.14), channel_id=1, source_target_pairs={{0,16},{16,0},{1,17},{17,1},{2,18},{18,2},{3,19},{19,3},{4,20},{20... | collective-permute-start | bytes 1572872 | tf_op jit(solution)/shard_map/ppermute | solution.py:320
  45.5 0.8 %shard_map.45 = (f32[64,2,7,2,128]{4,3,2,1,0:T(2,128)}, f32[2,128]{1,0:T(2,128)S(1)}) custom-call(f32[64,8,2,128]{3,2,1,0:T(2,128)S(1)} %bitcast.15), custom_call_target="tpu_custom_call" | custom-call | flops 10000000 | bytes 917504 | tf_op jit(solution)/shard_map/pallas_call | solution.py:322
  46.3 0.7 %collective-permute-done.1.other_ref = f32[64,8,2,128]{3,2,1,0:T(2,128)S(1)} collective-permute-done((f32[64,8,2,128]{3,2,1,0:T(2,128)S(1)}, f32[64,8,2,128]{3,2,1,0:T(2,128)S(1)}, u32[]{:S(2)}, u32[]{:S(2)}) %collective-permute-start.1) | collective-permute-done | bytes 524320 | tf_op jit(solution)/shard_map/ppermute | solution.py:320
  47.0 0.8 %shard_map.46 = (f32[64,2,7,2,128]{4,3,2,1,0:T(2,128)}, f32[3]{0:T(128)}) custom-call(f32[2,128]{1,0:T(2,128)S(1)} %get-tuple-element.20.worst_ref, f32[64,8,2,128]{3,2,1,0:T(2,128)S(1)} %collective-permute-done.1.other_ref, f32[64,2,7,2,128]{4,3,2,1,0:T(2,128)} %get-tuple-element.21._), custom_call_target="tpu_custom_call", output_to_operand_aliasing={{0}: (2, {})} | custom-call | tf_op jit(solution)/shard_map/pallas_call | solution.py:330
  (1 shorter events, 0.0 us)
Async XLA Ops:
  25.8 0.7 %copy-start = (s32[3]{0:T(128)S(1)}, s32[3]{0:T(128)}, u32[]{:S(2)}) copy-start(s32[3]{0:T(128)} %plan_ref.1) | copy-start | bytes 40
  25.9 1.7 %collective-permute-start = (f32[4,112,128]{2,1,0:T(8,128)S(1)}, f32[4,112,128]{2,1,0:T(8,128)S(1)}, u32[]{:S(2)}, u32[]{:S(2)}) collective-permute-start(f32[4,112,128]{2,1,0:T(8,128)S(1)} %shard_map.41.own_ref), channel_id=1, source_target_pairs={{0,16},{16,0},{1,17},{17,1},{2,18},{18,2},{3,19},{19,3},{4,20},{20... | collective-permute-start | bytes 688136 | tf_op jit(solution)/shard_map/ppermute | solution.py:289
  43.9 3.1 %collective-permute-start.1 = (f32[64,8,2,128]{3,2,1,0:T(2,128)S(1)}, f32[64,8,2,128]{3,2,1,0:T(2,128)S(1)}, u32[]{:S(2)}, u32[]{:S(2)}) collective-permute-start(f32[64,8,2,128]{3,2,1,0:T(2,128)S(1)} %bitcast.14), channel_id=1, source_target_pairs={{0,16},{16,0},{1,17},{17,1},{2,18},{18,2},{3,19},{19,3},{4,20},{20... | collective-permute-start | bytes 1572872 | tf_op jit(solution)/shard_map/ppermute | solution.py:320

commit v8 on v7

--- a/solution.py
+++ b/solution.py
@@ -137,14 +137,18 @@
         far_ref[i] = most(worst)
 
 
-def wanted(plan_ref, mask_ref, plan_here, plan_sem):
-    asked = pltpu.make_async_copy(plan_ref, plan_here, plan_sem)
-    asked.start()
-    asked.wait()
-    a, b, c = plan_here[0], plan_here[1], plan_here[2]
+def wanted(plan_ref, mask_ref):
+    plan = plan_ref[...]
+    place = lax.broadcasted_iota(jnp.int32, plan.shape, 1)
+    a, b, c = (
+        jnp.sum(jnp.where(place == i, plan, 0), axis=1, keepdims=True)
+        for i in range(3)
+    )
     for i in range(mask_ref.shape[0]):
         asked = (i == a) | (i == 3 + 3 * a + b) | (i == 12 + c)
-        mask_ref[i] = jnp.full((8, COLS), jnp.where(asked, 1.0, 0.0))
+        mask_ref[i] = jnp.broadcast_to(
+            jnp.where(asked, 1.0, 0.0), mask_ref.shape[1:]
+        )
 
 
 def folded(mask_ref, choices):
@@ -300,14 +304,10 @@
     mask = kernel(
         wanted,
         out_shape=real((15, 8, COLS)),
-        in_specs=[hbm],
+        in_specs=[vmem],
         out_specs=vmem,
-        scratch_shapes=[
-            pltpu.SMEM(plan.shape, plan.dtype),
-            pltpu.SemaphoreType.DMA,
-        ],
         cost_estimate=under_swap,
-    )(plan)
+    )(plan.reshape(1, -1))
     share = kernel(
         together,
         out_shape=real((chips, CARRIED, COLS)),

time: 48.1 us -> 48.1 us (level)
  transfers between devices with their start and end apart: 2 -> 2, of which waited for: 2 -> 2; matrix products, arithmetic and copies ran while one was open for 0% -> 0% of each run, Pallas kernels for 4% -> 3%
where the time goes in v8:
time: 48.1 us; the launch traced here: 47.8 us
  blocking collectives  41.2 us (86%)
  Pallas kernels  2.39 us (5%)
  starting transfers between devices  2.2 us (5%)
  waiting for transfers between devices  1.35 us (3%)
  between operations  0.67 us (1%)
    all_to_all x1, blocking collectives, on_device(): lax.all_to_all(entries, PLANE, 0, 0, tiled=True, axis_index_groups=members)  25.2 us
    all_to_all x1, blocking collectives, on_device(): lax.all_to_all(share, PLANE, 0, 0, tiled=True, axis_index_groups=members)  16 us
    ppermute x1, starting transfers between devices, on_device(): other = lax.ppermute(own, 'core', cores)  1.6 us
  transfers between devices with their start and end apart: 2, of which 2 were waited for; matrix products, arithmetic and copies ran while one was open for 0% of the time, Pallas kernels for 3%

profile of v8, /device:TPU:1, one launch (start us, length us, event | category | flops | bytes accessed | tf_op | source)
XLA Modules:
  0.0 47.8 jit_solution(4335318150881696161)
XLA Ops:
  0.6 25.2 %all_to_all.10 = f32[64,14,2,128]{3,2,1,0:T(2,128)S(1)} all-to-all(f32[64,14,2,128]{3,2,1,0:T(2,128)} %bitcast.18), channel_id=1, replica_groups={{73,75,72,74,65,67,64,66,69,71,68,70,77,79,76,78,9,11,8,10,1,3,0,2,5,7,..., dimensions={0} | all-to-all | bytes 1835008 | tf_op jit(solution)/shard_map/all_to_all | solution.py:286
  25.9 0.0 copy-start
  25.9 0.6 %collective-permute-start = (f32[4,112,128]{2,1,0:T(8,128)S(1)}, f32[4,112,128]{2,1,0:T(8,128)S(1)}, u32[]{:S(2)}, u32[]{:S(2)}) collective-permute-start(f32[4,112,128]{2,1,0:T(8,128)S(1)} %shard_map.41.own_ref), channel_id=1, source_target_pairs={{0,16},{16,0},{1,17},{17,1},{2,18},{18,2},{3,19},{19,3},{4,20},{20... | collective-permute-start | bytes 688136 | tf_op jit(solution)/shard_map/ppermute | solution.py:293
  26.5 0.1 copy-done
  26.5 0.1 shard_map.43.mask_ref
  26.6 0.3 shard_map.42
  27.0 0.6 %collective-permute-done.other_ref = f32[4,112,128]{2,1,0:T(8,128)S(1)} collective-permute-done((f32[4,112,128]{2,1,0:T(8,128)S(1)}, f32[4,112,128]{2,1,0:T(8,128)S(1)}, u32[]{:S(2)}, u32[]{:S(2)}) %collective-permute-start) | collective-permute-done | bytes 229408 | tf_op jit(solution)/shard_map/ppermute | solution.py:293
  27.6 0.3 shard_map.44
  27.9 16.0 %all_to_all.11 = f32[64,16,128]{2,1,0:T(8,128)S(1)} all-to-all(f32[64,16,128]{2,1,0:T(8,128)S(1)} %shard_map.44), channel_id=1, replica_groups={{73,75,72,74,65,67,64,66,69,71,68,70,77,79,76,78,9,11,8,10,1,3,0,2,5,7,..., dimensions={0} | all-to-all | bytes 1048576 | tf_op jit(solution)/shard_map/all_to_all | solution.py:317
  43.9 1.6 %collective-permute-start.1 = (f32[64,8,2,128]{3,2,1,0:T(2,128)S(1)}, f32[64,8,2,128]{3,2,1,0:T(2,128)S(1)}, u32[]{:S(2)}, u32[]{:S(2)}) collective-permute-start(f32[64,8,2,128]{3,2,1,0:T(2,128)S(1)} %bitcast.15), channel_id=1, source_target_pairs={{0,16},{16,0},{1,17},{17,1},{2,18},{18,2},{3,19},{19,3},{4,20},{20... | collective-permute-start | bytes 1572872 | tf_op jit(solution)/shard_map/ppermute | solution.py:320
  45.5 0.8 %shard_map.45 = (f32[64,2,7,2,128]{4,3,2,1,0:T(2,128)}, f32[2,128]{1,0:T(2,128)S(1)}) custom-call(f32[64,8,2,128]{3,2,1,0:T(2,128)S(1)} %bitcast.16), custom_call_target="tpu_custom_call" | custom-call | flops 10000000 | bytes 917504 | tf_op jit(solution)/shard_map/pallas_call | solution.py:322
  46.3 0.7 %collective-permute-done.1.other_ref = f32[64,8,2,128]{3,2,1,0:T(2,128)S(1)} collective-permute-done((f32[64,8,2,128]{3,2,1,0:T(2,128)S(1)}, f32[64,8,2,128]{3,2,1,0:T(2,128)S(1)}, u32[]{:S(2)}, u32[]{:S(2)}) %collective-permute-start.1) | collective-permute-done | bytes 524320 | tf_op jit(solution)/shard_map/ppermute | solution.py:320
  47.0 0.8 %shard_map.46 = (f32[64,2,7,2,128]{4,3,2,1,0:T(2,128)}, f32[3]{0:T(128)}) custom-call(f32[2,128]{1,0:T(2,128)S(1)} %get-tuple-element.20.worst_ref, f32[64,8,2,128]{3,2,1,0:T(2,128)S(1)} %collective-permute-done.1.other_ref, f32[64,2,7,2,128]{4,3,2,1,0:T(2,128)} %get-tuple-element.21._), custom_call_target="tpu_custom_call", output_to_operand_aliasing={{0}: (2, {})} | custom-call | tf_op jit(solution)/shard_map/pallas_call | solution.py:330
  (1 shorter events, 0.0 us)
Async XLA Ops:
  25.9 0.7 %copy-start = (s32[3]{0:T(128)S(1)}, s32[3]{0:T(128)}, u32[]{:S(2)}) copy-start(s32[3]{0:T(128)} %param.3) | copy-start | bytes 40
  25.9 1.7 %collective-permute-start = (f32[4,112,128]{2,1,0:T(8,128)S(1)}, f32[4,112,128]{2,1,0:T(8,128)S(1)}, u32[]{:S(2)}, u32[]{:S(2)}) collective-permute-start(f32[4,112,128]{2,1,0:T(8,128)S(1)} %shard_map.41.own_ref), channel_id=1, source_target_pairs={{0,16},{16,0},{1,17},{17,1},{2,18},{18,2},{3,19},{19,3},{4,20},{20... | collective-permute-start | bytes 688136 | tf_op jit(solution)/shard_map/ppermute | solution.py:293
  43.9 3.1 %collective-permute-start.1 = (f32[64,8,2,128]{3,2,1,0:T(2,128)S(1)}, f32[64,8,2,128]{3,2,1,0:T(2,128)S(1)}, u32[]{:S(2)}, u32[]{:S(2)}) collective-permute-start(f32[64,8,2,128]{3,2,1,0:T(2,128)S(1)} %bitcast.15), channel_id=1, source_target_pairs={{0,16},{16,0},{1,17},{17,1},{2,18},{18,2},{3,19},{19,3},{4,20},{20... | collective-permute-start | bytes 1572872 | tf_op jit(solution)/shard_map/ppermute | solution.py:320

commit v9 on v8

--- a/solution.py
+++ b/solution.py
@@ -8,7 +8,7 @@
 from jax.sharding import Mesh
 from jax.sharding import PartitionSpec as P
 
-PLANE = ("z", "y", "x_hi", "x_lo")
+PLANE = ("y", "z", "x_hi", "x_lo")
 YZ_ORDER, X_ORDER = (2, 0, 1, 3), (2, 3, 0, 1)
 COLS = 128
 CHIP = 28
@@ -77,7 +77,7 @@
             y,
             [
                 functools.reduce(
-                    jnp.add, [tile(g_ref, 4 * z + y, t) for z in range(4)]
+                    jnp.add, [tile(g_ref, 4 * y + z, t) for z in range(4)]
                 )
                 for t in range(2 * SIDE)
             ],
@@ -94,13 +94,13 @@
         for t in range(SIDE):
             mz = []
             for half in (t, t + SIDE):
-                values = [tile(g_ref, 4 * z + y, half) for z in range(4)]
+                values = [tile(g_ref, 4 * y + z, half) for z in range(4)]
                 _, top, bottom = stats(values)
                 high.append(top)
                 low.append(bottom)
             for z in range(4):
-                a = tile(g_ref, 4 * z + y, t)
-                mean = (a + tile(g_ref, 4 * z + y, t + SIDE)) * 0.5
+                a = tile(g_ref, 4 * y + z, t)
+                mean = (a + tile(g_ref, 4 * y + z, t + SIDE)) * 0.5
                 dev_z.append(jnp.abs(a - mean))
                 mz.append(mean)
             _, top, bottom = stats(mz)
@@ -115,7 +115,7 @@
     dev_y, y_yz = [], []
     for z in range(4):
         found = [
-            stats([tile(g_ref, 4 * z + y, t) for y in range(4)])
+            stats([tile(g_ref, 4 * y + z, t) for y in range(4)])
             for t in range(2 * SIDE)
         ]
         my = over_gy([f[0] for f in found])
@@ -126,7 +126,7 @@
         y_yz.append(most(gaps(my[:ONE], myz)))
         for t in range(SIDE):
             mz = [
-                (tile(g_ref, 4 * z + y, t) + tile(g_ref, 4 * z + y, t + SIDE))
+                (tile(g_ref, 4 * y + z, t) + tile(g_ref, 4 * y + z, t + SIDE))
                 * 0.5
                 for y in range(4)
             ]
@@ -278,7 +278,7 @@
     )
     cores = [(0, 1), (1, 0)]
     members = [
-        [16 * z + 4 * y + x for z in YZ_ORDER for y in YZ_ORDER for x in X_ORDER]
+        [16 * y + 4 * z + x for y in YZ_ORDER for z in YZ_ORDER for x in X_ORDER]
     ]
 
     entries = grads.reshape(rows // 8, 8, tiles, COLS).transpose(0, 2, 1, 3)
@@ -324,7 +324,7 @@
         out_shape=(whole, real((2, COLS))),
         in_specs=[vmem],
         out_specs=(hbm, vmem),
-        scratch_shapes=[pltpu.SemaphoreType.DMA((2,))],
+        scratch_shapes=[pltpu.SemaphoreType.DMA((1,))],
         cost_estimate=under_swap,
     )(own)
     whole, reports = kernel(
@@ -334,7 +334,7 @@
         out_specs=(hbm, hbm),
         scratch_shapes=[
             pltpu.SMEM((3,), jnp.float32),
-            pltpu.SemaphoreType.DMA((2,)),
+            pltpu.SemaphoreType.DMA((1,)),
             pltpu.SemaphoreType.DMA,
         ],
         input_output_aliases={2: 0},

time: 48.1 us -> 48.1 us (level)
  starting transfers between devices: 2.2 us -> 3.32 us
  blocking collectives: 41.2 us -> 40.1 us
    ppermute x1, starting transfers between devices: 0.6 us -> 1.7 us  [on_device(): other_sum = lax.ppermute(own_sum, 'core', cores)]
    all_to_all x1, blocking collectives: 25.2 us -> 24.3 us  [on_device(): lax.all_to_all(entries, PLANE, 0, 0, tiled=True, axis_index_groups=members)]
where the time goes in v9:
time: 48.1 us; the launch traced here: 47.9 us
  blocking collectives  40.1 us (83%)
  starting transfers between devices  3.32 us (7%)
  Pallas kernels  2.38 us (5%)
  waiting for transfers between devices  1.4 us (3%)
  between operations  0.67 us (1%)
    all_to_all x1, blocking collectives, on_device(): lax.all_to_all(entries, PLANE, 0, 0, tiled=True, axis_index_groups=members)  24.3 us
    all_to_all x1, blocking collectives, on_device(): lax.all_to_all(share, PLANE, 0, 0, tiled=True, axis_index_groups=members)  15.8 us
    ppermute x1, starting transfers between devices, on_device(): other_sum = lax.ppermute(own_sum, 'core', cores)  1.7 us
    ppermute x1, starting transfers between devices, on_device(): other = lax.ppermute(own, 'core', cores)  1.62 us
  transfers between devices with their start and end apart: 2, of which 2 were waited for; matrix products, arithmetic and copies ran while one was open for 0% of the time, Pallas kernels for 3%

profile of v9, /device:TPU:1, one launch (start us, length us, event | category | flops | bytes accessed | tf_op | source)
XLA Modules:
  0.0 47.9 jit_solution(3837172991922577329)
XLA Ops:
  0.6 24.3 %all_to_all.10 = f32[64,14,2,128]{3,2,1,0:T(2,128)S(1)} all-to-all(f32[64,14,2,128]{3,2,1,0:T(2,128)} %bitcast.18), channel_id=1, replica_groups={{73,75,72,74,9,11,8,10,41,43,40,42,105,107,104,106,65,67,64,66,1,3,0,2,..., dimensions={0} | all-to-all | bytes 1835008 | tf_op jit(solution)/shard_map/all_to_all | solution.py:286
  24.9 0.0 copy-start
  25.0 1.7 %collective-permute-start = (f32[4,112,128]{2,1,0:T(8,128)S(1)}, f32[4,112,128]{2,1,0:T(8,128)S(1)}, u32[]{:S(2)}, u32[]{:S(2)}) collective-permute-start(f32[4,112,128]{2,1,0:T(8,128)S(1)} %shard_map.41.own_ref), channel_id=1, source_target_pairs={{0,16},{16,0},{1,17},{17,1},{2,18},{18,2},{3,19},{19,3},{4,20},{20... | collective-permute-start | bytes 688136 | tf_op jit(solution)/shard_map/ppermute | solution.py:293
  26.7 0.0 copy-done
  26.7 0.1 shard_map.43.mask_ref
  26.8 0.3 shard_map.42
  27.1 0.7 %collective-permute-done.other_ref = f32[4,112,128]{2,1,0:T(8,128)S(1)} collective-permute-done((f32[4,112,128]{2,1,0:T(8,128)S(1)}, f32[4,112,128]{2,1,0:T(8,128)S(1)}, u32[]{:S(2)}, u32[]{:S(2)}) %collective-permute-start) | collective-permute-done | bytes 229408 | tf_op jit(solution)/shard_map/ppermute | solution.py:293
  27.8 0.3 shard_map.44
  28.1 15.8 %all_to_all.11 = f32[64,16,128]{2,1,0:T(8,128)S(1)} all-to-all(f32[64,16,128]{2,1,0:T(8,128)S(1)} %shard_map.44), channel_id=1, replica_groups={{73,75,72,74,9,11,8,10,41,43,40,42,105,107,104,106,65,67,64,66,1,3,0,2,..., dimensions={0} | all-to-all | bytes 1048576 | tf_op jit(solution)/shard_map/all_to_all | solution.py:317
  43.9 1.6 %collective-permute-start.1 = (f32[64,8,2,128]{3,2,1,0:T(2,128)S(1)}, f32[64,8,2,128]{3,2,1,0:T(2,128)S(1)}, u32[]{:S(2)}, u32[]{:S(2)}) collective-permute-start(f32[64,8,2,128]{3,2,1,0:T(2,128)S(1)} %bitcast.15), channel_id=1, source_target_pairs={{0,16},{16,0},{1,17},{17,1},{2,18},{18,2},{3,19},{19,3},{4,20},{20... | collective-permute-start | bytes 1572872 | tf_op jit(solution)/shard_map/ppermute | solution.py:320
  45.5 0.8 %shard_map.45 = (f32[64,2,7,2,128]{4,3,2,1,0:T(2,128)}, f32[2,128]{1,0:T(2,128)S(1)}) custom-call(f32[64,8,2,128]{3,2,1,0:T(2,128)S(1)} %bitcast.16), custom_call_target="tpu_custom_call" | custom-call | flops 10000000 | bytes 917504 | tf_op jit(solution)/shard_map/pallas_call | solution.py:322
  46.3 0.7 %collective-permute-done.1.other_ref = f32[64,8,2,128]{3,2,1,0:T(2,128)S(1)} collective-permute-done((f32[64,8,2,128]{3,2,1,0:T(2,128)S(1)}, f32[64,8,2,128]{3,2,1,0:T(2,128)S(1)}, u32[]{:S(2)}, u32[]{:S(2)}) %collective-permute-start.1) | collective-permute-done | bytes 524320 | tf_op jit(solution)/shard_map/ppermute | solution.py:320
  47.1 0.8 %shard_map.46 = (f32[64,2,7,2,128]{4,3,2,1,0:T(2,128)}, f32[3]{0:T(128)}) custom-call(f32[2,128]{1,0:T(2,128)S(1)} %get-tuple-element.20.worst_ref, f32[64,8,2,128]{3,2,1,0:T(2,128)S(1)} %collective-permute-done.1.other_ref, f32[64,2,7,2,128]{4,3,2,1,0:T(2,128)} %get-tuple-element.21._), custom_call_target="tpu_custom_call", output_to_operand_aliasing={{0}: (2, {})} | custom-call | tf_op jit(solution)/shard_map/pallas_call | solution.py:330
  (1 shorter events, 0.0 us)
Async XLA Ops:
  24.9 1.7 %copy-start = (s32[3]{0:T(128)S(1)}, s32[3]{0:T(128)}, u32[]{:S(2)}) copy-start(s32[3]{0:T(128)} %param.3) | copy-start | bytes 40
  25.0 2.8 %collective-permute-start = (f32[4,112,128]{2,1,0:T(8,128)S(1)}, f32[4,112,128]{2,1,0:T(8,128)S(1)}, u32[]{:S(2)}, u32[]{:S(2)}) collective-permute-start(f32[4,112,128]{2,1,0:T(8,128)S(1)} %shard_map.41.own_ref), channel_id=1, source_target_pairs={{0,16},{16,0},{1,17},{17,1},{2,18},{18,2},{3,19},{19,3},{4,20},{20... | collective-permute-start | bytes 688136 | tf_op jit(solution)/shard_map/ppermute | solution.py:293
  43.9 3.2 %collective-permute-start.1 = (f32[64,8,2,128]{3,2,1,0:T(2,128)S(1)}, f32[64,8,2,128]{3,2,1,0:T(2,128)S(1)}, u32[]{:S(2)}, u32[]{:S(2)}) collective-permute-start(f32[64,8,2,128]{3,2,1,0:T(2,128)S(1)} %bitcast.15), channel_id=1, source_target_pairs={{0,16},{16,0},{1,17},{17,1},{2,18},{18,2},{3,19},{19,3},{4,20},{20... | collective-permute-start | bytes 1572872 | tf_op jit(solution)/shard_map/ppermute | solution.py:320
